TPU v7x, 128 devices: a whole 4x4x4 slice. The times are simulated.
128 devices in a mesh: gx: 2 (over core), gy: 64 (over z, y, x).
Axes of the slice: x: 4, y: 4, z: 4, core: 2. Of those that a mesh axis runs over, the one named last changes fastest.
Arguments:
- right_side: float32 [128, 16384], P('gx', 'gy'), may hold values from -34 to 34, as said below
- initial: float32 [128, 16384], P('gx', 'gy'), may hold values from -0.6 to 0.6
- reaction: float32 [128, 16384], P('gx', 'gy'), may hold values from 0.05 to 0.5
- velocity_x: float32 [128, 16384], P('gx', 'gy'), may hold values from -1 to 1
- velocity_y: float32 [128, 16384], P('gx', 'gy'), may hold values from -1 to 1
Outputs:
- solution: float32 [128, 16384], P('gx', 'gy')
- residual: float32 [128, 16384], P('gx', 'gy')
Inputs may be any that keep to these rules, and one draw needn't show every extreme that they name: right_side is noise bounded by 4 in size times an envelope 0.5 + 8 g, where g is a periodic Gaussian bump of one device block's width along each dimension centred at a drawn position, so its entries lie within -34 and 34.
All inputs are finite; a program needn't handle non-finite values.
Results may differ from a plain program's by a relative error of at most 0.0075.
Values sent between devices are 32-bit elements.
A program may use at most 64 MiB of HBM per device.

v0:
```python
import jax
import jax.numpy as jnp
from jax import lax
from jax.sharding import Mesh
from jax.sharding import PartitionSpec as P

RESTART = 15
GX_GY = ("gx", "gy_0", "gy_1", "gy_2")
GY = ("gy_0", "gy_1", "gy_2")


def padded_2(cells, sides, width, closed):
    for axis, dim in sides:
        count = lax.axis_size(axis)
        ends = count if closed else count - 1
        head = lax.slice_in_dim(cells, 0, width, axis=dim)
        tail = lax.slice_in_dim(cells, cells.shape[dim] - width, cells.shape[dim], axis=dim)
        cells = jnp.concatenate(
            [
                lax.ppermute(tail, axis, [(i, (i + 1) % count) for i in range(ends)]),
                cells,
                lax.ppermute(head, axis, [((i + 1) % count, i) for i in range(ends)]),
            ],
            axis=dim,
        )
    return cells


def one_axis_at_a_time(x, axes):
    for axis in axes:
        x = lax.psum(x, axis)
    return x


def shifted(padded, offset, dimension, extent):
    row_start = 2 + offset if dimension == 0 else 2
    column_start = 2 + offset if dimension == 1 else 2
    return lax.slice(
        padded, (row_start, column_start), (row_start + extent[0], column_start + extent[1])
    )


def first_diff(padded, dimension, extent):
    outer = shifted(padded, -2, dimension, extent) - shifted(padded, 2, dimension, extent)
    inner = shifted(padded, 1, dimension, extent) - shifted(padded, -1, dimension, extent)
    return (outer + 8.0 * inner) / 12.0


def second_diff(padded, dimension, extent):
    inner = shifted(padded, 1, dimension, extent) + shifted(padded, -1, dimension, extent)
    outer = shifted(padded, 2, dimension, extent) + shifted(padded, -2, dimension, extent)
    return (16.0 * inner - outer - 30.0 * shifted(padded, 0, dimension, extent)) / 12.0


def apply_operator(field, padded_field, padded_speeds, reaction, velocity_x, velocity_y):
    extent = field.shape
    diffusion = second_diff(padded_field, 0, extent) + second_diff(padded_field, 1, extent)
    advect_x = 0.5 * (
        velocity_x * first_diff(padded_field, 0, extent)
        + first_diff(padded_speeds[0] * padded_field, 0, extent)
    )
    advect_y = 0.5 * (
        velocity_y * first_diff(padded_field, 1, extent)
        + first_diff(padded_speeds[1] * padded_field, 1, extent)
    )
    return reaction * field - diffusion + advect_x + advect_y


def least_squares(hessenberg, beta):
    columns_total = hessenberg.shape[1]
    target = jnp.where(jnp.arange(columns_total + 1) == 0, beta, 0.0)

    def rotate(column, carried):
        upper, target = carried
        top_row = upper[column]
        next_row = upper[column + 1]
        diagonal_entry = top_row[column]
        below_entry = next_row[column]
        radius = jnp.sqrt(diagonal_entry * diagonal_entry + below_entry * below_entry)
        cosine = diagonal_entry / radius
        sine_value = below_entry / radius
        upper = upper.at[column].set(cosine * top_row + sine_value * next_row)
        upper = upper.at[column + 1].set(cosine * next_row - sine_value * top_row)
        upper_value = target[column]
        lower_value = target[column + 1]
        target = target.at[column].set(cosine * upper_value + sine_value * lower_value)
        target = target.at[column + 1].set(cosine * lower_value - sine_value * upper_value)
        return (upper, target)

    upper, target = lax.fori_loop(0, columns_total, rotate, (hessenberg, target))

    def substitute(count, weights):
        row_index = columns_total - 1 - count
        known = jnp.sum(upper[row_index] * weights)
        return weights.at[row_index].set((target[row_index] - known) / upper[row_index, row_index])

    return lax.fori_loop(0, columns_total, substitute, jnp.zeros((columns_total,), jnp.float32))


def per_device(right_side, initial, reaction, velocity_x, velocity_y):
    row_count, column_count = right_side.shape
    speeds = jnp.stack([velocity_x, velocity_y])
    padded_speeds = padded_2(speeds, (("gx", 1), (GY, 2)), 2, True)

    def operator_on(field):
        padded_field = padded_2(field, (("gx", 0), (GY, 1)), 2, True)
        return apply_operator(field, padded_field, padded_speeds, reaction, velocity_x, velocity_y)

    start_residual = right_side - operator_on(initial)
    start_square = one_axis_at_a_time(jnp.sum(start_residual * start_residual), GX_GY)
    beta = jnp.sqrt(start_square)
    basis = jnp.zeros((RESTART + 1, row_count, column_count), jnp.float32)
    basis = basis.at[0].set(start_residual / beta)
    hessenberg = jnp.zeros((RESTART + 1, RESTART), jnp.float32)
    positions = jnp.arange(RESTART + 1)

    def arnoldi(column, carried):
        basis, hessenberg = carried
        current = lax.dynamic_index_in_dim(basis, column, 0, keepdims=False)
        applied = operator_on(current)
        local_projection = jnp.einsum("kxy,xy->k", basis, applied, precision=lax.Precision.HIGHEST)
        projection, applied_square = (
            one_axis_at_a_time(local_projection, GX_GY),
            one_axis_at_a_time(jnp.sum(applied * applied), GX_GY),
        )
        applied = applied - jnp.einsum(
            "k,kxy->xy", projection, basis, precision=lax.Precision.HIGHEST
        )
        length = jnp.sqrt(applied_square - jnp.sum(projection * projection))
        entries = jnp.where(positions == column + 1, length, projection)
        hessenberg = lax.dynamic_update_slice(hessenberg, entries[:, None], (0, column))
        basis = lax.dynamic_update_index_in_dim(basis, applied / length, column + 1, 0)
        return (basis, hessenberg)

    basis, hessenberg = lax.fori_loop(0, RESTART, arnoldi, (basis, hessenberg))
    weights = least_squares(hessenberg, beta)
    padded_weights = jnp.concatenate([weights, jnp.zeros((1,), jnp.float32)])
    solution = initial + jnp.einsum(
        "k,kxy->xy", padded_weights, basis, precision=lax.Precision.HIGHEST
    )
    leftover = jnp.where(positions == 0, beta, 0.0) - jnp.dot(
        hessenberg, weights, precision=lax.Precision.HIGHEST
    )
    residual = jnp.einsum("k,kxy->xy", leftover, basis, precision=lax.Precision.HIGHEST)
    return (solution, residual)


def solution(mesh):
    torus = Mesh(mesh.devices.reshape(mesh.shape["gx"], 4, 4, 4), ("gx", "gy_0", "gy_1", "gy_2"))
    placed = (P("gx", GY), P("gx", GY), P("gx", GY), P("gx", GY), P("gx", GY))
    return jax.shard_map(
        per_device,
        mesh=torus,
        in_specs=placed,
        out_specs=(P("gx", GY), P("gx", GY)),
        check_vma=False,
    )
```

profile of v0, /device:TPU:1, one launch (start us, length us, event | category | flops | bytes accessed | tf_op | source)
XLA Modules:
  0.0 1030.0 jit_solution(6680681950074222786)
XLA Ops:
  4.6 8.6 collective-permute-start.6
  13.4 7.0 collective-permute-start.11
  29.4 6.7 psum.141
  42.7 13.4 %psum.143 = f32[]{:T(128)} all-reduce(f32[]{:T(128)} %psum.142), channel_id=1, replica_groups=mesh['gx'=2,'gy_0'=4,'gy_1'=4,'gy_2'=4] {'gy_2'}, use_global_device_ids=true, to_apply=%region_4.0 | all-reduce | flops 1 | bytes 8 | tf_op jit(solution)/shard_map/psum | solution.py:31
  56.8 747.0 %while.56 = (s32[]{:T(128)}, f32[16,64,256]{2,1,0:T(8,128)S(1)}, f32[16,15]{0,1:T(8,128)S(1)}, f32[64,256]{1,0:T(8,128)S(1)}, f32[64,256]{1,0:T(8,128)S(1)}, /*i...) while((s32[]{:T(128)}, f32[16,64,256]{2,1,0:T(8,128)S(1)}, ...), condition=%wide.region_16.0_spmd.clone, body=%wide.region_5.16_spmd.clone.sunk | while | flops 7373337 | bytes 4410527 | solution.py:135
  79.9 6.7 all-reduce.10
  86.6 6.6 all-reduce.11
  93.2 6.7 all-reduce.12
  115.5 7.2 collective-permute-done.3
  129.9 6.7 all-reduce.10
  136.6 6.6 all-reduce.11
  143.2 6.8 all-reduce.12
  165.6 7.2 collective-permute-done.3
  180.0 6.7 all-reduce.10
  186.7 6.6 all-reduce.11
  193.3 6.8 all-reduce.12
  215.6 7.2 collective-permute-done.3
  230.0 6.7 all-reduce.10
  236.7 6.6 all-reduce.11
  243.3 6.8 all-reduce.12
  265.7 7.2 collective-permute-done.3
  280.1 6.7 all-reduce.10
  286.8 6.6 all-reduce.11
  293.4 6.8 all-reduce.12
  315.7 7.2 collective-permute-done.3
  330.1 6.7 all-reduce.10
  336.8 6.6 all-reduce.11
  343.4 6.8 all-reduce.12
  365.8 7.2 collective-permute-done.3
  380.2 6.7 all-reduce.10
  386.9 6.6 all-reduce.11
  393.5 6.8 all-reduce.12
  415.8 7.2 collective-permute-done.3
  430.2 6.7 all-reduce.10
  436.9 6.6 all-reduce.11
  443.5 6.8 all-reduce.12
  465.9 7.2 collective-permute-done.3
  480.3 6.7 all-reduce.10
  487.0 6.6 all-reduce.11
  493.6 6.8 all-reduce.12
  515.9 7.2 collective-permute-done.3
  530.3 6.7 all-reduce.10
  537.0 6.6 all-reduce.11
  543.6 6.8 all-reduce.12
  566.0 7.2 collective-permute-done.3
  580.4 6.7 all-reduce.10
  587.1 6.6 all-reduce.11
  593.7 6.8 all-reduce.12
  616.0 7.2 collective-permute-done.3
  630.4 6.7 all-reduce.10
  637.1 6.6 all-reduce.11
  643.7 6.8 all-reduce.12
  666.1 7.2 collective-permute-done.3
  680.5 6.7 all-reduce.10
  693.8 6.8 all-reduce.12
  716.1 7.2 collective-permute-done.3
  730.5 6.7 all-reduce.10
  743.8 6.8 all-reduce.12
  766.2 7.2 collective-permute-done.3
  780.6 6.7 all-reduce.10
  787.3 6.6 all-reduce.11
  793.9 6.8 all-reduce.12
  804.5 162.3 %while.54 = (s32[]{:T(128)}, f32[16,15]{1,0:T(8,128)S(1)}, f32[16]{0:T(128)S(1)}, s32[]{:T(128)}, s32[2]{0:T(128)S(1)}, /*index=5*/s32[1]{0:T(128)}, s32[]{:T(128)}, s32[]{:T(128)}, s32[]{:T(128)}, s32[]{:T(128)}) while((s32[]{:T(128)}, f32[16,15]{1,0:T(8,128)S(1)}, f32[16]{0:T(128)S(1)}, s32[]{:T(128)}, s32[2]{0:T(128)S(1)}, ...), condition=%wide.region_20.21_spmd, body=%wide.region_17.20_spmd.sunk | while | flops 165 | bytes 5167 | solution.py:90
  966.8 59.4 %while.55 = (s32[]{:T(128)}, f32[15]{0:T(128)S(1)}, f32[16]{0:T(128)S(1)}, f32[16,15]{1,0:T(8,128)S(1)}, s32[]{:T(128)}, /*index=5*/s32[]{:T(128)}, s32[]{:T(128)}, s32[]{:T(128)}, s32[]{:T(128)}) while((s32[]{:T(128)}, f32[15]{0:T(128)S(1)}, f32[16]{0:T(128)S(1)}, f32[16,15]{1,0:T(8,128)S(1)}, s32[]{:T(128)}, /*index=5*/s32[]{:T(128)}, ...), condition=%wide.region_23.24_spmd, body=%wide.region_21.23_spmd.sunk | while | flops 43 | bytes 490 | solution.py:97
  (594 shorter events, 455.6 us)
Async XLA Ops:
  1.4 11.7 %collective-permute-start.8 = (f32[2,2,256]{2,1,0:T(2,128)S(1)}, f32[2,2,256]{2,1,0:T(2,128)S(1)}, u32[]{:S(2)}, u32[]{:S(2)}) collective-permute-start(f32[2,2,256]{2,1,0:T(2,128)S(1)} %get-tuple-element.581), channel_id=1, source_target_pairs={{0,64},{64,0},{1,65},{65,1},{2,66},{66,2},{3,67},{67,3},{4,68},{68... | collective-permute-start | bytes 12296 | tf_op jit(solution)/shard_map/ppermute | solution.py:20
  2.8 10.4 %collective-permute-start.9 = (f32[2,2,256]{2,1,0:T(2,128)S(1)}, f32[2,2,256]{2,1,0:T(2,128)S(1)}, u32[]{:S(2)}, u32[]{:S(2)}) collective-permute-start(f32[2,2,256]{2,1,0:T(2,128)S(1)} %get-tuple-element.582), channel_id=1, source_target_pairs={{64,0},{0,64},{65,1},{1,65},{66,2},{2,66},{67,3},{3,67},{68,4},{4,... | collective-permute-start | bytes 12296 | tf_op jit(solution)/shard_map/ppermute | solution.py:22
  2.9 1.3 collective-permute-start.4
  3.3 1.2 collective-permute-start.5
  4.6 15.7 %collective-permute-start.6 = (f32[68,2]{1,0:T(8,128)S(1)}, f32[68,2]{1,0:T(8,128)S(1)}, u32[]{:S(2)}, u32[]{:S(2)}) collective-permute-start(f32[68,2]{1,0:T(8,128)S(1)} %get-tuple-element.584), channel_id=1, source_target_pairs={{1,0},{2,1},{3,2},{4,3},{5,4},{6,5},{7,6},{8,7},{9,8},{10,9},{11,1... | collective-permute-start | bytes 1640 | tf_op jit(solution)/shard_map/ppermute | solution.py:22
  13.1 8.2 collective-permute-start.7
  13.3 9.4 collective-permute-start.10
  13.4 9.4 collective-permute-start.11
  56.9 7.3 collective-permute-start
  63.3 1.2 collective-permute-start.1
  64.6 2.8 collective-permute-start.2
  64.6 8.3 collective-permute-start.3
  103.2 7.3 collective-permute-start
  109.6 1.2 collective-permute-start.1
  110.9 4.6 collective-permute-start.2
  114.5 8.2 collective-permute-start.3
  153.2 7.3 collective-permute-start
  159.7 1.2 collective-permute-start.1
  161.0 4.6 collective-permute-start.2
  164.5 8.2 collective-permute-start.3
  203.3 7.3 collective-permute-start
  209.8 1.2 collective-permute-start.1
  211.0 4.6 collective-permute-start.2
  214.6 8.2 collective-permute-start.3
  253.3 7.3 collective-permute-start
  259.8 1.2 collective-permute-start.1
  261.1 4.6 collective-permute-start.2
  264.6 8.2 collective-permute-start.3
  303.4 7.3 collective-permute-start
  309.9 1.2 collective-permute-start.1
  311.1 4.6 collective-permute-start.2
  314.7 8.2 collective-permute-start.3
  353.4 7.3 collective-permute-start
  359.9 1.2 collective-permute-start.1
  361.2 4.6 collective-permute-start.2
  364.7 8.2 collective-permute-start.3
  403.5 7.3 collective-permute-start
  410.0 1.2 collective-permute-start.1
  411.2 4.6 collective-permute-start.2
  414.8 8.2 collective-permute-start.3
  453.5 7.3 collective-permute-start
  460.0 1.2 collective-permute-start.1
  461.3 4.6 collective-permute-start.2
  464.8 8.2 collective-permute-start.3
  503.6 7.3 collective-permute-start
  510.1 1.2 collective-permute-start.1
  511.3 4.6 collective-permute-start.2
  514.9 8.2 collective-permute-start.3
  553.6 7.3 collective-permute-start
  561.4 4.6 collective-permute-start.2
  564.9 8.2 collective-permute-start.3
  603.7 7.3 collective-permute-start
  611.4 4.6 collective-permute-start.2
  615.0 8.2 collective-permute-start.3
  653.7 7.3 collective-permute-start
  660.2 1.2 collective-permute-start.1
  661.5 4.6 collective-permute-start.2
  665.0 8.2 collective-permute-start.3
  703.8 7.3 collective-permute-start
  711.5 4.6 collective-permute-start.2
  715.1 8.2 collective-permute-start.3
  753.8 7.3 collective-permute-start
  761.6 4.6 collective-permute-start.2
  765.1 8.2 collective-permute-start.3
  (10 other events, 26.6 us)
where the time goes:
time: 1040 us; the launch traced here: 1030 us
  blocking collectives  398 us (38%)
  starting transfers between devices  167 us (16%)
  loops' own time  149 us (14%)
  waiting for transfers between devices  141 us (14%)
  other arithmetic  84.3 us (8%)
  matrix products  46.7 us (4%)
  local copies, waits for them, and re-layouts  42.3 us (4%)
    psum x64, blocking collectives, one_axis_at_a_time(): x = lax.psum(x, axis)  398 us
    ppermute x34, starting transfers between devices, padded_2(): lax.ppermute(head, axis, [((i + 1) % count, i) for i in range(ends)])  163 us
    ppermute x34, waiting for transfers between devices, padded_2(): lax.ppermute(tail, axis, [(i, (i + 1) % count) for i in range(ends)])  114 us
    another operation x1, loops' own time, least_squares(): lax.fori_loop(0, columns_total, rotate, (hessenberg, target))  97.8 us
    another operation x46, other arithmetic  30.6 us
    another operation x1, loops' own time, least_squares(): lax.fori_loop(0, columns_total, substitute, jnp.zeros((columns_total,), j...  30.2 us
    ppermute x34, waiting for transfers between devices, padded_2(): lax.ppermute(head, axis, [((i + 1) % count, i) for i in range(ends)])  27.7 us
    dot_general x15, matrix products, arnoldi(): jnp.einsum('kxy,xy->k', basis, applied, precision=lax.Precision.HIGHEST)  26.6 us
  transfers between devices with their start and end apart: 68, of which 64 were waited for; matrix products, arithmetic and copies ran while one was open for 0% of the time, Pallas kernels for 0%

commit v1 on v0

v1 whole, which is shorter than its diff:
```python
import functools
import itertools

import jax
import jax.numpy as jnp
from jax import lax
from jax.experimental import pallas as pl
from jax.experimental.pallas import tpu as pltpu
from jax.sharding import Mesh
from jax.sharding import PartitionSpec as P

RESTART = 15
VECTORS = RESTART + 1
GY = ("gy_0", "gy_1", "gy_2")
AXES = ("gx",) + GY
PHASES = (("gx", "gy_2"), ("gy_1",), ("gy_0",))
DEPTH = 32
GROUPS = 4
STEPS = 16
SHIFT, SCALE, BACK = 5.525, 2.72, 0.94
B, X0, RE, VX, VY = 0, 1, 2, 3, 4
PACKED = (X0, RE, VX, VY)


def values_at_zero():
    values = [1.0, -SHIFT / SCALE]
    for _ in range(VECTORS - 2):
        values.append(-(SHIFT / SCALE) * values[-1] - BACK * values[-2])
    return values


def kernel(sizes, *refs):
    inputs = refs[:5]
    outputs = refs[5:7]
    (block, pack, halo, coef, field, basis, mirror, gram_parts, out) = refs[7:16]
    phases = [p for p in PHASES if any(sizes[a] > 1 for a in p)]
    reduce_bufs = refs[16 : 16 + len(phases)]
    (load_sem, swap_sem, halo_send, halo_recv, mirror_sem, out_sem) = refs[
        16 + len(phases) : 22 + len(phases)
    ]
    reduce_sems = refs[22 + len(phases) :]

    place = {a: lax.axis_index(a) for a in AXES}
    core = place["gx"]
    sibling = {"gx": 1 - core}

    def along(step):
        total = sizes["gy_0"] * sizes["gy_1"] * sizes["gy_2"]
        flat = (place["gy_0"] * sizes["gy_1"] + place["gy_1"]) * sizes["gy_2"] + place["gy_2"]
        flat = lax.rem(flat + step + total, total)
        low = lax.rem(flat, sizes["gy_2"])
        rest = lax.div(flat, sizes["gy_2"])
        return lax.div(rest, sizes["gy_1"]), lax.rem(rest, sizes["gy_1"]), low

    right, left = along(1), along(-1)

    def at(chip, core_index):
        return {"gx": core_index, "gy_0": chip[0], "gy_1": chip[1], "gy_2": chip[2]}

    def group_of(axes):
        offsets = list(itertools.product(*[range(sizes[a]) for a in axes]))
        peers = []
        for offset in offsets:
            where = {a: lax.rem(place[a] + o, sizes[a]) for a, o in zip(axes, offset)}
            slot = 0
            for a in axes:
                slot = slot * sizes[a] + where[a]
            peers.append((where, slot))
        return peers

    groups = [group_of(axes) for axes in phases]

    loads = []
    for a in range(5):
        for tile in range(2):
            loads.append(
                pltpu.make_async_copy(
                    inputs[a].at[:, pl.ds(128 * tile, 128)],
                    block.at[a, tile, pl.ds(0, 64), :],
                    load_sem.at[a, tile],
                )
            )
            loads[-1].start()
    barrier = pltpu.get_barrier_semaphore()
    greeted = 0
    to_greet = [at(right, 0), at(right, 1), at(left, 0), at(left, 1), sibling]
    for group in groups:
        to_greet += [where for where, _ in group[1:]]
    for device in to_greet:
        pl.semaphore_signal(barrier, inc=1, device_id=device, device_id_type=pl.DeviceIdType.MESH)
        greeted += 1
    for load in loads:
        load.wait()

    lane = lax.broadcasted_iota(jnp.int32, (8, 128), 1)
    row = lax.broadcasted_iota(jnp.int32, (8, 128), 0)

    for i in range(8):
        rows = pl.ds(8 * i, 8)
        for side, tile, first in ((0, 1, 96), (1, 0, 0)):
            value = block[PACKED[0], tile, rows, :]
            for g in range(1, GROUPS):
                start = (first + DEPTH * g) % 128
                moved = pltpu.roll(block[PACKED[g], tile, rows, :], DEPTH * g, 1)
                inside = (lane >= start) & (lane < start + DEPTH)
                value = jnp.where(inside, moved, value)
            pack[side, rows, :] = value

    pl.semaphore_wait(barrier, greeted)

    swap = pltpu.make_async_remote_copy(
        block.at[:, :, pl.ds(0, 64), :],
        block.at[:, :, pl.ds(64, 64), :],
        swap_sem.at[0],
        swap_sem.at[1],
        device_id=sibling,
        device_id_type=pl.DeviceIdType.MESH,
    )
    swap.start()
    sends = []
    for side, chip, target in ((0, right, 0), (1, left, 1)):
        same = core if target == 0 else 1 - core
        for part in range(2):
            source = pack.at[side] if part == 0 else block.at[B, 1 - side, pl.ds(0, 64), :]
            copy = pltpu.make_async_remote_copy(
                source,
                halo.at[part, pl.ds(pl.multiple_of(64 * same, 64), 64), :],
                halo_send.at[side, part],
                halo_recv.at[part, same],
                device_id=at(chip, target),
                device_id_type=pl.DeviceIdType.MESH,
            )
            copy.start()
            sends.append(copy)
    swap.wait()
    for part in range(2):
        for half in range(2):
            pltpu.make_async_remote_copy(
                halo.at[part, pl.ds(64 * half, 64), :],
                halo.at[part, pl.ds(64 * half, 64), :],
                halo_send.at[0, part],
                halo_recv.at[part, half],
                device_id=sibling,
                device_id_type=pl.DeviceIdType.MESH,
            ).wait_recv()

    far = 1 - core
    first = jnp.where(core == 0, 96, 0)
    from_chip = (lane >= first) & (lane < first + DEPTH)
    for a in range(5):
        for t in range(STEPS):
            strided = pl.ds(t, 8, stride=STEPS)
            field[a, t, :, 0:128] = block[a, core, strided, :]
            if a == B:
                edge = halo[1, strided, :]
            else:
                g = PACKED.index(a)
                edge = halo[0, strided, :]
                if g:
                    edge = pltpu.roll(edge, 128 - DEPTH * g, 1)
            field[a, t, :, 128:256] = jnp.where(from_chip, edge, block[a, far, strided, :])

    def row_shift(load, t):
        if t >= STEPS:
            return pltpu.roll(load(t - STEPS), 7, 0)
        if t < 0:
            return pltpu.roll(load(t + STEPS), 1, 0)
        return load(t)

    def column_shift(value, offset):
        return pltpu.roll(value, (-offset) % 256, 1)

    inv = 1.0 / SCALE
    for t in range(STEPS):
        speed = lambda i: field[VX, i]
        here = speed(t)
        coef[0, t] = (field[RE, t] + (5.0 - SHIFT)) * inv
        coef[1, t] = (here + row_shift(speed, t + 1)) * (inv / 3.0) - 4.0 / 3.0 * inv
        coef[2, t] = (here + row_shift(speed, t - 1)) * (-inv / 3.0) - 4.0 / 3.0 * inv
        coef[3, t] = (here + row_shift(speed, t + 2)) * (-inv / 24.0) + inv / 12.0
        coef[4, t] = (here + row_shift(speed, t - 2)) * (inv / 24.0) + inv / 12.0
        here = field[VY, t]
        coef[5, t] = (here + column_shift(here, 1)) * (inv / 3.0) - 4.0 / 3.0 * inv
        coef[6, t] = (here + column_shift(here, -1)) * (-inv / 3.0) - 4.0 / 3.0 * inv
        coef[7, t] = (here + column_shift(here, 2)) * (-inv / 24.0) + inv / 12.0
        coef[8, t] = (here + column_shift(here, -2)) * (inv / 24.0) + inv / 12.0

    def operate(load, t):
        here = load(t)
        value = coef[0, t] * here
        value += coef[1, t] * row_shift(load, t + 1)
        value += coef[2, t] * row_shift(load, t - 1)
        value += coef[3, t] * row_shift(load, t + 2)
        value += coef[4, t] * row_shift(load, t - 2)
        value += coef[5, t] * column_shift(here, 1)
        value += coef[6, t] * column_shift(here, -1)
        value += coef[7, t] * column_shift(here, 2)
        value += coef[8, t] * column_shift(here, -2)
        return value

    for t in range(STEPS):
        load = lambda i: field[X0, i]
        basis[0, t] = jnp.zeros((8, 256), jnp.float32)
        basis[1, t] = field[B, t] - SCALE * operate(load, t) - SHIFT * load(t)

    def grow(k, carry):
        for t in range(STEPS):
            load = lambda i: basis[k + 1, i]
            basis[k + 2, t] = operate(load, t) - BACK * basis[k, t]
        return carry

    lax.fori_loop(0, RESTART, grow, 0)

    size = 4
    for bi in range(VECTORS // size):
        for bj in range(bi + 1):
            pairs = [
                (i, j)
                for i in range(bi * size, bi * size + size)
                for j in range(bj * size, bj * size + size)
                if j <= i
            ]
            sums = {}
            for t in range(STEPS):
                need = sorted({i for pair in pairs for i in pair})
                cells = {i: basis[i + 1, t, :, 0:128] for i in need}
                for i, j in pairs:
                    product = cells[i] * cells[j]
                    sums[i, j] = product if t == 0 else sums[i, j] + product
            for i, j in pairs:
                total = jnp.sum(sums[i, j], axis=0, keepdims=True)
                gram_parts[i, j : j + 1, :] = total
                if i != j:
                    gram_parts[j, i : i + 1, :] = total

    packed = jnp.zeros((8, 128), jnp.float32)
    for k in range(VECTORS):
        for half in range(2):
            total = jnp.sum(gram_parts[k, 8 * half : 8 * half + 8, :], axis=1, keepdims=True)
            packed = jnp.where(lane == 2 * k + half, total, packed)

    mirror_copy = pltpu.make_async_remote_copy(
        basis.at[pl.ds(1, VECTORS), :, :, pl.ds(0, 128)],
        mirror,
        mirror_sem.at[0],
        mirror_sem.at[1],
        device_id=sibling,
        device_id_type=pl.DeviceIdType.MESH,
    )
    for p, group in enumerate(groups):
        buf = reduce_bufs[p]
        send_sem, recv_sem = reduce_sems[2 * p], reduce_sems[2 * p + 1]
        mine = group[0][1]
        buf[mine] = packed
        copies = []
        for n, (where, slot) in enumerate(group[1:]):
            copy = pltpu.make_async_remote_copy(
                buf.at[mine],
                buf.at[mine],
                send_sem.at[n],
                recv_sem.at[mine],
                device_id=where,
                device_id_type=pl.DeviceIdType.MESH,
            )
            copy.start()
            copies.append(copy)
        if p == 0:
            mirror_copy.start()
        for n, (where, slot) in enumerate(group[1:]):
            pltpu.make_async_remote_copy(
                buf.at[slot],
                buf.at[slot],
                send_sem.at[n],
                recv_sem.at[slot],
                device_id=where,
                device_id_type=pl.DeviceIdType.MESH,
            ).wait_recv()
        packed = buf[0]
        for slot in range(1, len(group)):
            packed = packed + buf[slot]
        sends += copies
    mirror_copy.wait()

    values = values_at_zero()
    columns = []
    for k in range(VECTORS):
        columns.append(
            [
                jnp.broadcast_to(packed[:, 2 * k + h : 2 * k + h + 1], (8, 128))
                for h in range(2)
            ]
        )
    start = []
    for h in range(2):
        value = jnp.full((8, 128), values[8 * h], jnp.float32)
        for s in range(1, 8):
            value = jnp.where(row == s, values[8 * h + s], value)
        start.append(value)
    columns.append(list(start))

    def entry(column, i):
        return jnp.broadcast_to(column[i // 8][i % 8 : i % 8 + 1, :], (8, 128))

    for k in range(VECTORS):
        pivot = columns[k]
        inverse = 1.0 / entry(pivot, k)
        for j in range(k + 1, VECTORS + 1):
            factor = (entry(pivot, j) if j < VECTORS else entry(columns[j], k)) * inverse
            for h in range(2):
                columns[j][h] = columns[j][h] - pivot[h] * factor
            columns[j][k // 8] = jnp.where(row == k % 8, factor, columns[j][k // 8])
    u = columns[VECTORS]
    norm = jnp.sum(start[0] * u[0] + start[1] * u[1], axis=0, keepdims=True)
    inverse = jnp.broadcast_to(1.0 / norm, (8, 128))
    left_over = [entry(u, j) * inverse for j in range(VECTORS)]
    weights = [None] * RESTART
    for j in range(RESTART, 0, -1):
        value = left_over[j] * (-1.0 / SCALE)
        if j + 1 < RESTART:
            value = value - BACK * weights[j + 1]
        if j < RESTART:
            value = value - (SHIFT / SCALE) * weights[j]
        weights[j - 1] = value

    for t in range(STEPS):
        strided = pl.ds(t, 8, stride=STEPS)
        near = row < 4
        answer = jnp.where(
            near, block[X0, core, strided, :], pltpu.roll(block[X0, far, strided, :], 4, 0)
        )
        residual = jnp.zeros((8, 128), jnp.float32)
        for k in range(VECTORS):
            cells = jnp.where(near, basis[k + 1, t, :, 0:128], mirror[k, t])
            residual = residual + left_over[k] * cells
            if k < RESTART:
                answer = answer + weights[k] * cells
        out[0, strided, :] = answer
        out[1, strided, :] = residual

    stores = []
    for o in range(2):
        for part in range(2):
            tile = core if part == 0 else far
            copy = pltpu.make_async_copy(
                out.at[o, pl.ds(64 * part, 64), :],
                outputs[o].at[:, pl.ds(pl.multiple_of(128 * tile, 128), 128)],
                out_sem.at[o, part],
            )
            copy.start()
            stores.append(copy)
    for copy in sends:
        copy.wait_send()
    for copy in stores:
        copy.wait()


def per_device(sizes, *arrays):
    phases = [p for p in PHASES if any(sizes[a] > 1 for a in p)]
    counts = []
    for axes in phases:
        count = 1
        for a in axes:
            count *= sizes[a]
        counts.append(count)
    f32 = jnp.float32
    dma = pltpu.SemaphoreType.DMA
    reduce_sems = []
    for count in counts:
        reduce_sems += [dma((count,)), dma((count,))]
    shape = jax.ShapeDtypeStruct((64, 256), f32)
    return pl.pallas_call(
        functools.partial(kernel, sizes),
        out_shape=(shape, shape),
        in_specs=[pl.BlockSpec(memory_space=pl.ANY)] * 5,
        out_specs=(pl.BlockSpec(memory_space=pl.ANY),) * 2,
        scratch_shapes=[
            pltpu.VMEM((5, 2, 128, 128), f32),
            pltpu.VMEM((2, 64, 128), f32),
            pltpu.VMEM((2, 128, 128), f32),
            pltpu.VMEM((9, STEPS, 8, 256), f32),
            pltpu.VMEM((5, STEPS, 8, 256), f32),
            pltpu.VMEM((VECTORS + 1, STEPS, 8, 256), f32),
            pltpu.VMEM((VECTORS, STEPS, 8, 128), f32),
            pltpu.VMEM((VECTORS, VECTORS, 128), f32),
            pltpu.VMEM((2, 128, 128), f32),
        ]
        + [pltpu.VMEM((count, 8, 128), f32) for count in counts]
        + [
            dma((5, 2)),
            dma((2,)),
            dma((2, 2)),
            dma((2, 2)),
            dma((2,)),
            dma((2, 2)),
        ]
        + reduce_sems,
        compiler_params=pltpu.CompilerParams(collective_id=0, has_side_effects=True),
    )(*arrays)


def solution(mesh):
    counts = (4, 4, 4) if mesh.shape["gy"] == 64 else (1, 2, mesh.shape["gy"] // 2)
    torus = Mesh(mesh.devices.reshape((mesh.shape["gx"],) + counts), AXES)
    spec = P("gx", GY)
    return jax.shard_map(
        functools.partial(per_device, dict(torus.shape)),
        mesh=torus,
        in_specs=(spec,) * 5,
        out_specs=(spec, spec),
        check_vma=False,
    )
```

time: 1040 us -> 33.4 us (0.03)
  the two profiles are of different devices: /device:TPU:1 before, /device:TPU:0 now
where the time goes in v1:
time: 33.4 us; the launch traced here: 33.2 us
  Pallas kernels  30.4 us (91%)
  local copies, waits for them, and re-layouts  2.14 us (6%)
  between operations  0.65 us (2%)
    pallas_call x1, Pallas kernels, per_device(): pl.pallas_call(functools.partial(kernel, sizes), out_shape=(shape, shape)...  30.4 us
    unnamed x4, local copies, waits for them, and re-layouts  2.14 us

profile of v1, /device:TPU:0, one launch (start us, length us, event | category | flops | bytes accessed | tf_op | source)
XLA Modules:
  0.0 33.2 jit_solution(10793394642983934644)
XLA Ops:
  0.6 30.4 %shard_map.68 = (f32[64,256]{1,0:T(8,128)}, f32[64,256]{1,0:T(8,128)}) custom-call(f32[64,256]{1,0:T(8,128)} %refs_0_.1, f32[64,256]{1,0:T(8,128)} %refs_1_.1, f32[64,256]{1,0:T(8,128)} %refs_2_.1, f32[64,256]{1,0:T(8,128)} %refs_3_.1, f32[64,256]{1,0:T(8,128)} %refs_4_.1), custom_call_target="tpu_custom_call" | custom-call | tf_op jit(solution)/shard_map/pallas_call | solution.py:371
  31.1 0.0 copy-start
  31.1 1.5 %copy.9 = f32[64,256]{1,0:T(8,128)} copy(f32[64,256]{1,0:T(8,128)} %get-tuple-element.4) | data formatting | bytes 131072
  32.6 0.0 copy-done
  32.6 0.6 %copy.10 = f32[64,256]{1,0:T(8,128)} copy(f32[64,256]{1,0:T(8,128)S(1)} %copy-done) | data formatting | bytes 131072
Async XLA Ops:
  31.1 1.5 %copy-start = (f32[64,256]{1,0:T(8,128)S(1)}, f32[64,256]{1,0:T(8,128)}, u32[]{:S(2)}) copy-start(f32[64,256]{1,0:T(8,128)} %get-tuple-element.5) | copy-start | bytes 196612

commit v2 on v1

--- a/solution.py
+++ b/solution.py
@@ -1,5 +1,4 @@
 import functools
-import itertools
 
 import jax
 import jax.numpy as jnp
@@ -13,7 +12,7 @@
 VECTORS = RESTART + 1
 GY = ("gy_0", "gy_1", "gy_2")
 AXES = ("gx",) + GY
-PHASES = (("gx", "gy_2"), ("gy_1",), ("gy_0",))
+LOGICAL = pl.DeviceIdType.LOGICAL
 DEPTH = 32
 GROUPS = 4
 STEPS = 16
@@ -33,12 +32,11 @@
     inputs = refs[:5]
     outputs = refs[5:7]
     (block, pack, halo, coef, field, basis, mirror, gram_parts, out) = refs[7:16]
-    phases = [p for p in PHASES if any(sizes[a] > 1 for a in p)]
-    reduce_bufs = refs[16 : 16 + len(phases)]
-    (load_sem, swap_sem, halo_send, halo_recv, mirror_sem, out_sem) = refs[
-        16 + len(phases) : 22 + len(phases)
-    ]
-    reduce_sems = refs[22 + len(phases) :]
+    (gathered, share) = refs[16:18]
+    (load_sem, swap_sem, halo_send, halo_recv, mirror_sem, out_sem, send_sem, recv_sem) = refs[18:]
+    devices = 1
+    for a in AXES:
+        devices *= sizes[a]
 
     place = {a: lax.axis_index(a) for a in AXES}
     core = place["gx"]
@@ -57,18 +55,9 @@
     def at(chip, core_index):
         return {"gx": core_index, "gy_0": chip[0], "gy_1": chip[1], "gy_2": chip[2]}
 
-    def group_of(axes):
-        offsets = list(itertools.product(*[range(sizes[a]) for a in axes]))
-        peers = []
-        for offset in offsets:
-            where = {a: lax.rem(place[a] + o, sizes[a]) for a, o in zip(axes, offset)}
-            slot = 0
-            for a in axes:
-                slot = slot * sizes[a] + where[a]
-            peers.append((where, slot))
-        return peers
-
-    groups = [group_of(axes) for axes in phases]
+    me = core
+    for a in GY:
+        me = me * sizes[a] + place[a]
 
     loads = []
     for a in range(5):
@@ -82,13 +71,10 @@
             )
             loads[-1].start()
     barrier = pltpu.get_barrier_semaphore()
-    greeted = 0
-    to_greet = [at(right, 0), at(right, 1), at(left, 0), at(left, 1), sibling]
-    for group in groups:
-        to_greet += [where for where, _ in group[1:]]
-    for device in to_greet:
-        pl.semaphore_signal(barrier, inc=1, device_id=device, device_id_type=pl.DeviceIdType.MESH)
-        greeted += 1
+    for o in range(1, devices):
+        pl.semaphore_signal(
+            barrier, inc=1, device_id=lax.rem(me + o, devices), device_id_type=LOGICAL
+        )
     for load in loads:
         load.wait()
 
@@ -106,7 +92,7 @@
                 value = jnp.where(inside, moved, value)
             pack[side, rows, :] = value
 
-    pl.semaphore_wait(barrier, greeted)
+    pl.semaphore_wait(barrier, devices - 1)
 
     swap = pltpu.make_async_remote_copy(
         block.at[:, :, pl.ds(0, 64), :],
@@ -233,12 +219,26 @@
                 if i != j:
                     gram_parts[j, i : i + 1, :] = total
 
+    place_in = lane - 32 * (row & 3)
     packed = jnp.zeros((8, 128), jnp.float32)
     for k in range(VECTORS):
         for half in range(2):
             total = jnp.sum(gram_parts[k, 8 * half : 8 * half + 8, :], axis=1, keepdims=True)
-            packed = jnp.where(lane == 2 * k + half, total, packed)
-
+            packed = jnp.where(place_in == 2 * k + half, total, packed)
+    for r in range(2):
+        line = jnp.sum(packed[4 * r : 4 * r + 4, :], axis=0, keepdims=True)
+        share[r : r + 1, :] = line
+        gathered[me, r : r + 1, :] = line
+
+    for o in range(1, devices):
+        pltpu.make_async_remote_copy(
+            share,
+            gathered.at[me],
+            send_sem,
+            recv_sem,
+            device_id=lax.rem(me + o, devices),
+            device_id_type=LOGICAL,
+        ).start()
     mirror_copy = pltpu.make_async_remote_copy(
         basis.at[pl.ds(1, VECTORS), :, :, pl.ds(0, 128)],
         mirror,
@@ -247,38 +247,18 @@
         device_id=sibling,
         device_id_type=pl.DeviceIdType.MESH,
     )
-    for p, group in enumerate(groups):
-        buf = reduce_bufs[p]
-        send_sem, recv_sem = reduce_sems[2 * p], reduce_sems[2 * p + 1]
-        mine = group[0][1]
-        buf[mine] = packed
-        copies = []
-        for n, (where, slot) in enumerate(group[1:]):
-            copy = pltpu.make_async_remote_copy(
-                buf.at[mine],
-                buf.at[mine],
-                send_sem.at[n],
-                recv_sem.at[mine],
-                device_id=where,
-                device_id_type=pl.DeviceIdType.MESH,
-            )
-            copy.start()
-            copies.append(copy)
-        if p == 0:
-            mirror_copy.start()
-        for n, (where, slot) in enumerate(group[1:]):
-            pltpu.make_async_remote_copy(
-                buf.at[slot],
-                buf.at[slot],
-                send_sem.at[n],
-                recv_sem.at[slot],
-                device_id=where,
-                device_id_type=pl.DeviceIdType.MESH,
-            ).wait_recv()
-        packed = buf[0]
-        for slot in range(1, len(group)):
-            packed = packed + buf[slot]
-        sends += copies
+    mirror_copy.start()
+    others = gathered.at[pl.ds(0, devices - 1)]
+    everyone = pltpu.make_async_remote_copy(
+        others, others, send_sem, recv_sem, device_id=sibling, device_id_type=pl.DeviceIdType.MESH
+    )
+    everyone.wait_recv()
+    summed = jnp.sum(gathered[...], axis=0)
+    summed = jnp.where(
+        row < 4,
+        jnp.broadcast_to(summed[0:1, :], (8, 128)),
+        jnp.broadcast_to(summed[1:2, :], (8, 128)),
+    )
     mirror_copy.wait()
 
     values = values_at_zero()
@@ -286,7 +266,12 @@
     for k in range(VECTORS):
         columns.append(
             [
-                jnp.broadcast_to(packed[:, 2 * k + h : 2 * k + h + 1], (8, 128))
+                jnp.broadcast_to(
+                    jnp.sum(
+                        jnp.where(place_in == 2 * k + h, summed, 0.0), axis=1, keepdims=True
+                    ),
+                    (8, 128),
+                )
                 for h in range(2)
             ]
         )
@@ -348,6 +333,7 @@
             )
             copy.start()
             stores.append(copy)
+    everyone.wait_send()
     for copy in sends:
         copy.wait_send()
     for copy in stores:
@@ -355,18 +341,11 @@
 
 
 def per_device(sizes, *arrays):
-    phases = [p for p in PHASES if any(sizes[a] > 1 for a in p)]
-    counts = []
-    for axes in phases:
-        count = 1
-        for a in axes:
-            count *= sizes[a]
-        counts.append(count)
+    devices = 1
+    for a in AXES:
+        devices *= sizes[a]
     f32 = jnp.float32
     dma = pltpu.SemaphoreType.DMA
-    reduce_sems = []
-    for count in counts:
-        reduce_sems += [dma((count,)), dma((count,))]
     shape = jax.ShapeDtypeStruct((64, 256), f32)
     return pl.pallas_call(
         functools.partial(kernel, sizes),
@@ -383,17 +362,17 @@
             pltpu.VMEM((VECTORS, STEPS, 8, 128), f32),
             pltpu.VMEM((VECTORS, VECTORS, 128), f32),
             pltpu.VMEM((2, 128, 128), f32),
-        ]
-        + [pltpu.VMEM((count, 8, 128), f32) for count in counts]
-        + [
+            pltpu.VMEM((devices, 2, 128), f32),
+            pltpu.VMEM((2, 128), f32),
             dma((5, 2)),
             dma((2,)),
             dma((2, 2)),
             dma((2, 2)),
             dma((2,)),
             dma((2, 2)),
-        ]
-        + reduce_sems,
+            dma,
+            dma,
+        ],
         compiler_params=pltpu.CompilerParams(collective_id=0, has_side_effects=True),
     )(*arrays)
 

time: 33.4 us -> 30.5 us (0.913)
  the two profiles are of different devices: /device:TPU:0 before, /device:TPU:1 now
where the time goes in v2:
time: 30.5 us; the launch traced here: 30.4 us
  Pallas kernels  27.6 us (90%)
  local copies, waits for them, and re-layouts  2.14 us (7%)
  between operations  0.65 us (2%)
    pallas_call x1, Pallas kernels, per_device(): pl.pallas_call(functools.partial(kernel, sizes), out_shape=(shape, shape)...  27.6 us
    unnamed x4, local copies, waits for them, and re-layouts  2.14 us

profile of v2, /device:TPU:1, one launch (start us, length us, event | category | flops | bytes accessed | tf_op | source)
XLA Modules:
  0.0 30.4 jit_solution(8152015893466088142)
XLA Ops:
  0.6 27.6 %shard_map.68 = (f32[64,256]{1,0:T(8,128)}, f32[64,256]{1,0:T(8,128)}) custom-call(f32[64,256]{1,0:T(8,128)} %refs_0_.1, f32[64,256]{1,0:T(8,128)} %refs_1_.1, f32[64,256]{1,0:T(8,128)} %refs_2_.1, f32[64,256]{1,0:T(8,128)} %refs_3_.1, f32[64,256]{1,0:T(8,128)} %refs_4_.1), custom_call_target="tpu_custom_call" | custom-call | tf_op jit(solution)/shard_map/pallas_call | solution.py:350
  28.2 0.0 copy-start
  28.2 1.5 %copy.9 = f32[64,256]{1,0:T(8,128)} copy(f32[64,256]{1,0:T(8,128)} %get-tuple-element.4) | data formatting | bytes 131072
  29.7 0.0 copy-done
  29.7 0.6 %copy.10 = f32[64,256]{1,0:T(8,128)} copy(f32[64,256]{1,0:T(8,128)S(1)} %copy-done) | data formatting | bytes 131072
Async XLA Ops:
  28.2 1.5 %copy-start = (f32[64,256]{1,0:T(8,128)S(1)}, f32[64,256]{1,0:T(8,128)}, u32[]{:S(2)}) copy-start(f32[64,256]{1,0:T(8,128)} %get-tuple-element.5) | copy-start | bytes 196612

commit v3 on v2

--- a/solution.py
+++ b/solution.py
@@ -16,7 +16,7 @@
 DEPTH = 32
 GROUPS = 4
 STEPS = 16
-SHIFT, SCALE, BACK = 5.525, 2.72, 0.94
+SHIFT, SCALE = 5.525, 2.65
 B, X0, RE, VX, VY = 0, 1, 2, 3, 4
 PACKED = (X0, RE, VX, VY)
 
@@ -24,16 +24,18 @@
 def values_at_zero():
     values = [1.0, -SHIFT / SCALE]
     for _ in range(VECTORS - 2):
-        values.append(-(SHIFT / SCALE) * values[-1] - BACK * values[-2])
+        values.append(-(SHIFT / SCALE) * values[-1] - values[-2])
     return values
 
 
 def kernel(sizes, *refs):
     inputs = refs[:5]
-    outputs = refs[5:7]
-    (block, pack, halo, coef, field, basis, mirror, gram_parts, out) = refs[7:16]
-    (gathered, share) = refs[16:18]
-    (load_sem, swap_sem, halo_send, halo_recv, mirror_sem, out_sem, send_sem, recv_sem) = refs[18:]
+    out = refs[5]
+    (block, pack, halo, halo_b, edge_b, coef, field, basis, merged, mirror, gram_parts) = refs[
+        6:17
+    ]
+    (gathered, share) = refs[17:19]
+    (load_sem, swap_sem, halo_send, halo_recv, mirror_sem, send_sem, recv_sem) = refs[19:]
     devices = 1
     for a in AXES:
         devices *= sizes[a]
@@ -73,7 +75,7 @@
     barrier = pltpu.get_barrier_semaphore()
     for o in range(1, devices):
         pl.semaphore_signal(
-            barrier, inc=1, device_id=lax.rem(me + o, devices), device_id_type=LOGICAL
+            barrier, inc=1, device_id=lax.bitwise_and(me + o, devices - 1), device_id_type=LOGICAL
         )
     for load in loads:
         load.wait()
@@ -91,6 +93,15 @@
                 inside = (lane >= start) & (lane < start + DEPTH)
                 value = jnp.where(inside, moved, value)
             pack[side, rows, :] = value
+    for i in range(2):
+        for side, tile, first in ((0, 1, 96), (1, 0, 0)):
+            value = block[B, tile, pl.ds(8 * i, 8), :]
+            for g in range(1, GROUPS):
+                start = (first + DEPTH * g) % 128
+                moved = pltpu.roll(block[B, tile, pl.ds(16 * g + 8 * i, 8), :], DEPTH * g, 1)
+                inside = (lane >= start) & (lane < start + DEPTH)
+                value = jnp.where(inside, moved, value)
+            pack[side, pl.ds(64 + 8 * i, 8), :] = value
 
     pl.semaphore_wait(barrier, devices - 1)
 
@@ -107,10 +118,15 @@
     for side, chip, target in ((0, right, 0), (1, left, 1)):
         same = core if target == 0 else 1 - core
         for part in range(2):
-            source = pack.at[side] if part == 0 else block.at[B, 1 - side, pl.ds(0, 64), :]
+            if part == 0:
+                source = pack.at[side, pl.ds(0, 64), :]
+                landing = halo.at[pl.ds(pl.multiple_of(64 * same, 64), 64), :]
+            else:
+                source = pack.at[side, pl.ds(64, 16), :]
+                landing = halo_b.at[pl.ds(pl.multiple_of(16 * same, 16), 16), :]
             copy = pltpu.make_async_remote_copy(
                 source,
-                halo.at[part, pl.ds(pl.multiple_of(64 * same, 64), 64), :],
+                landing,
                 halo_send.at[side, part],
                 halo_recv.at[part, same],
                 device_id=at(chip, target),
@@ -118,33 +134,8 @@
             )
             copy.start()
             sends.append(copy)
-    swap.wait()
-    for part in range(2):
-        for half in range(2):
-            pltpu.make_async_remote_copy(
-                halo.at[part, pl.ds(64 * half, 64), :],
-                halo.at[part, pl.ds(64 * half, 64), :],
-                halo_send.at[0, part],
-                halo_recv.at[part, half],
-                device_id=sibling,
-                device_id_type=pl.DeviceIdType.MESH,
-            ).wait_recv()
-
     far = 1 - core
-    first = jnp.where(core == 0, 96, 0)
-    from_chip = (lane >= first) & (lane < first + DEPTH)
-    for a in range(5):
-        for t in range(STEPS):
-            strided = pl.ds(t, 8, stride=STEPS)
-            field[a, t, :, 0:128] = block[a, core, strided, :]
-            if a == B:
-                edge = halo[1, strided, :]
-            else:
-                g = PACKED.index(a)
-                edge = halo[0, strided, :]
-                if g:
-                    edge = pltpu.roll(edge, 128 - DEPTH * g, 1)
-            field[a, t, :, 128:256] = jnp.where(from_chip, edge, block[a, far, strided, :])
+    inv = 1.0 / SCALE
 
     def row_shift(load, t):
         if t >= STEPS:
@@ -154,48 +145,92 @@
         return load(t)
 
     def column_shift(value, offset):
-        return pltpu.roll(value, (-offset) % 256, 1)
-
-    inv = 1.0 / SCALE
+        return pltpu.roll(value, (-offset) % 128, 1)
+
+    def build(q, first, edge):
+        inside = (lane >= first) & (lane < first + DEPTH)
+        for a in range(5):
+            for t in range(STEPS):
+                strided = pl.ds(t, 8, stride=STEPS)
+                field[a, q, t] = jnp.where(inside, edge(a, strided), block[a, core, strided, :])
+        for t in range(STEPS):
+            speed = lambda i: field[VX, q, i]
+            here = speed(t)
+            coef[0, q, t] = (field[RE, q, t] + (5.0 - SHIFT)) * inv
+            coef[1, q, t] = (here + row_shift(speed, t + 1)) * (inv / 3.0) - 4.0 / 3.0 * inv
+            coef[2, q, t] = (here + row_shift(speed, t - 1)) * (-inv / 3.0) - 4.0 / 3.0 * inv
+            coef[3, q, t] = (here + row_shift(speed, t + 2)) * (-inv / 24.0) + inv / 12.0
+            coef[4, q, t] = (here + row_shift(speed, t - 2)) * (inv / 24.0) + inv / 12.0
+            here = field[VY, q, t]
+            coef[5, q, t] = (here + column_shift(here, 1)) * (inv / 3.0) - 4.0 / 3.0 * inv
+            coef[6, q, t] = (here + column_shift(here, -1)) * (-inv / 3.0) - 4.0 / 3.0 * inv
+            coef[7, q, t] = (here + column_shift(here, 2)) * (-inv / 24.0) + inv / 12.0
+            coef[8, q, t] = (here + column_shift(here, -2)) * (inv / 24.0) + inv / 12.0
+
+    swap.wait()
+    build(1 - core, 96 * core, lambda a, strided: block[a, far, strided, :])
+
+    for part, ref, count in ((0, halo, 64), (1, halo_b, 16)):
+        for half in range(2):
+            landing = ref.at[pl.ds(count * half, count), :]
+            pltpu.make_async_remote_copy(
+                landing,
+                landing,
+                halo_send.at[0, part],
+                halo_recv.at[part, half],
+                device_id=sibling,
+                device_id_type=pl.DeviceIdType.MESH,
+            ).wait_recv()
+    for s in range(8):
+        for i in range(2):
+            value = halo_b[pl.ds(16 * (s // 4) + 8 * i, 8), :]
+            if s % 4:
+                value = pltpu.roll(value, 128 - DEPTH * (s % 4), 1)
+            edge_b[pl.ds(16 * s + 8 * i, 8), :] = value
+
+    def from_chip(a, strided):
+        if a == B:
+            return edge_b[strided, :]
+        g = PACKED.index(a)
+        edge = halo[strided, :]
+        return pltpu.roll(edge, 128 - DEPTH * g, 1) if g else edge
+
+    build(core, 96 * (1 - core), from_chip)
+
+    def operate(load, q, t):
+        here = load(t)
+        value = coef[0, q, t] * here
+        value += coef[1, q, t] * row_shift(load, t + 1)
+        value += coef[2, q, t] * row_shift(load, t - 1)
+        value += coef[3, q, t] * row_shift(load, t + 2)
+        value += coef[4, q, t] * row_shift(load, t - 2)
+        value += coef[5, q, t] * column_shift(here, 1)
+        value += coef[6, q, t] * column_shift(here, -1)
+        value += coef[7, q, t] * column_shift(here, 2)
+        value += coef[8, q, t] * column_shift(here, -2)
+        return value
+
+    own_left = lane < 64
     for t in range(STEPS):
-        speed = lambda i: field[VX, i]
-        here = speed(t)
-        coef[0, t] = (field[RE, t] + (5.0 - SHIFT)) * inv
-        coef[1, t] = (here + row_shift(speed, t + 1)) * (inv / 3.0) - 4.0 / 3.0 * inv
-        coef[2, t] = (here + row_shift(speed, t - 1)) * (-inv / 3.0) - 4.0 / 3.0 * inv
-        coef[3, t] = (here + row_shift(speed, t + 2)) * (-inv / 24.0) + inv / 12.0
-        coef[4, t] = (here + row_shift(speed, t - 2)) * (inv / 24.0) + inv / 12.0
-        here = field[VY, t]
-        coef[5, t] = (here + column_shift(here, 1)) * (inv / 3.0) - 4.0 / 3.0 * inv
-        coef[6, t] = (here + column_shift(here, -1)) * (-inv / 3.0) - 4.0 / 3.0 * inv
-        coef[7, t] = (here + column_shift(here, 2)) * (-inv / 24.0) + inv / 12.0
-        coef[8, t] = (here + column_shift(here, -2)) * (inv / 24.0) + inv / 12.0
-
-    def operate(load, t):
-        here = load(t)
-        value = coef[0, t] * here
-        value += coef[1, t] * row_shift(load, t + 1)
-        value += coef[2, t] * row_shift(load, t - 1)
-        value += coef[3, t] * row_shift(load, t + 2)
-        value += coef[4, t] * row_shift(load, t - 2)
-        value += coef[5, t] * column_shift(here, 1)
-        value += coef[6, t] * column_shift(here, -1)
-        value += coef[7, t] * column_shift(here, 2)
-        value += coef[8, t] * column_shift(here, -2)
-        return value
-
-    for t in range(STEPS):
-        load = lambda i: field[X0, i]
-        basis[0, t] = jnp.zeros((8, 256), jnp.float32)
-        basis[1, t] = field[B, t] - SCALE * operate(load, t) - SHIFT * load(t)
+        parts = []
+        for q in range(2):
+            load = lambda i: field[X0, q, i]
+            basis[0, q, t] = jnp.zeros((8, 128), jnp.float32)
+            parts.append(field[B, q, t] - SCALE * operate(load, q, t) - SHIFT * load(t))
+            basis[1, q, t] = parts[q]
+        merged[0, t] = jnp.where(own_left, parts[0], parts[1])
 
     def grow(k, carry):
         for t in range(STEPS):
-            load = lambda i: basis[k + 1, i]
-            basis[k + 2, t] = operate(load, t) - BACK * basis[k, t]
+            parts = []
+            for q in range(2):
+                load = lambda i: basis[k + 1, q, i]
+                parts.append(operate(load, q, t) - basis[k, q, t])
+                basis[k + 2, q, t] = parts[q]
+            merged[k + 1, t] = jnp.where(own_left, parts[0], parts[1])
         return carry
 
-    lax.fori_loop(0, RESTART, grow, 0)
+    lax.fori_loop(0, RESTART, grow, 0, unroll=RESTART)
 
     size = 4
     for bi in range(VECTORS // size):
@@ -209,7 +244,7 @@
             sums = {}
             for t in range(STEPS):
                 need = sorted({i for pair in pairs for i in pair})
-                cells = {i: basis[i + 1, t, :, 0:128] for i in need}
+                cells = {i: merged[i, t] for i in need}
                 for i, j in pairs:
                     product = cells[i] * cells[j]
                     sums[i, j] = product if t == 0 else sums[i, j] + product
@@ -236,11 +271,11 @@
             gathered.at[me],
             send_sem,
             recv_sem,
-            device_id=lax.rem(me + o, devices),
+            device_id=lax.bitwise_and(me + o, devices - 1),
             device_id_type=LOGICAL,
         ).start()
     mirror_copy = pltpu.make_async_remote_copy(
-        basis.at[pl.ds(1, VECTORS), :, :, pl.ds(0, 128)],
+        merged,
         mirror,
         mirror_sem.at[0],
         mirror_sem.at[1],
@@ -302,7 +337,7 @@
     for j in range(RESTART, 0, -1):
         value = left_over[j] * (-1.0 / SCALE)
         if j + 1 < RESTART:
-            value = value - BACK * weights[j + 1]
+            value = value - weights[j + 1]
         if j < RESTART:
             value = value - (SHIFT / SCALE) * weights[j]
         weights[j - 1] = value
@@ -315,27 +350,31 @@
         )
         residual = jnp.zeros((8, 128), jnp.float32)
         for k in range(VECTORS):
-            cells = jnp.where(near, basis[k + 1, t, :, 0:128], mirror[k, t])
+            cells = jnp.where(near, merged[k, t], mirror[k, t])
             residual = residual + left_over[k] * cells
             if k < RESTART:
                 answer = answer + weights[k] * cells
         out[0, strided, :] = answer
         out[1, strided, :] = residual
 
+    everyone.wait_send()
+    for copy in sends:
+        copy.wait_send()
+
+
+def put_out(tiles, first, second, sem):
+    core = lax.axis_index("gx")
     stores = []
-    for o in range(2):
+    for o, output in enumerate((first, second)):
         for part in range(2):
-            tile = core if part == 0 else far
+            tile = core if part == 0 else 1 - core
             copy = pltpu.make_async_copy(
-                out.at[o, pl.ds(64 * part, 64), :],
-                outputs[o].at[:, pl.ds(pl.multiple_of(128 * tile, 128), 128)],
-                out_sem.at[o, part],
+                tiles.at[o, pl.ds(64 * part, 64), :],
+                output.at[:, pl.ds(pl.multiple_of(128 * tile, 128), 128)],
+                sem.at[o, part],
             )
             copy.start()
             stores.append(copy)
-    everyone.wait_send()
-    for copy in sends:
-        copy.wait_send()
     for copy in stores:
         copy.wait()
 
@@ -347,21 +386,23 @@
     f32 = jnp.float32
     dma = pltpu.SemaphoreType.DMA
     shape = jax.ShapeDtypeStruct((64, 256), f32)
-    return pl.pallas_call(
+    tiles = pl.pallas_call(
         functools.partial(kernel, sizes),
-        out_shape=(shape, shape),
+        out_shape=pltpu.VMEM((2, 128, 128), f32),
         in_specs=[pl.BlockSpec(memory_space=pl.ANY)] * 5,
-        out_specs=(pl.BlockSpec(memory_space=pl.ANY),) * 2,
+        out_specs=pl.BlockSpec(memory_space=pltpu.VMEM),
         scratch_shapes=[
             pltpu.VMEM((5, 2, 128, 128), f32),
-            pltpu.VMEM((2, 64, 128), f32),
-            pltpu.VMEM((2, 128, 128), f32),
-            pltpu.VMEM((9, STEPS, 8, 256), f32),
-            pltpu.VMEM((5, STEPS, 8, 256), f32),
-            pltpu.VMEM((VECTORS + 1, STEPS, 8, 256), f32),
+            pltpu.VMEM((2, 80, 128), f32),
+            pltpu.VMEM((128, 128), f32),
+            pltpu.VMEM((32, 128), f32),
+            pltpu.VMEM((128, 128), f32),
+            pltpu.VMEM((9, 2, STEPS, 8, 128), f32),
+            pltpu.VMEM((5, 2, STEPS, 8, 128), f32),
+            pltpu.VMEM((VECTORS + 1, 2, STEPS, 8, 128), f32),
+            pltpu.VMEM((VECTORS, STEPS, 8, 128), f32),
             pltpu.VMEM((VECTORS, STEPS, 8, 128), f32),
             pltpu.VMEM((VECTORS, VECTORS, 128), f32),
-            pltpu.VMEM((2, 128, 128), f32),
             pltpu.VMEM((devices, 2, 128), f32),
             pltpu.VMEM((2, 128), f32),
             dma((5, 2)),
@@ -369,12 +410,18 @@
             dma((2, 2)),
             dma((2, 2)),
             dma((2,)),
-            dma((2, 2)),
             dma,
             dma,
         ],
         compiler_params=pltpu.CompilerParams(collective_id=0, has_side_effects=True),
     )(*arrays)
+    return pl.pallas_call(
+        put_out,
+        out_shape=(shape, shape),
+        in_specs=[pl.BlockSpec(memory_space=pltpu.VMEM)],
+        out_specs=(pl.BlockSpec(memory_space=pl.ANY),) * 2,
+        scratch_shapes=[dma((2, 2))],
+    )(pltpu.with_memory_space_constraint(tiles, pltpu.VMEM))
 
 
 def solution(mesh):

time: 30.5 us -> 26.7 us (0.88)
  local copies, waits for them, and re-layouts: 2.14 us -> 0 us
  Pallas kernels: 27.6 us -> 25.9 us
    unnamed x4 -> x0, local copies, waits for them, and re-layouts: 2.14 us -> none
    pallas_call x1 -> x2, Pallas kernels: 27.6 us -> 25.9 us  [the longest x1 25.2 us: per_device(): pl.pallas_call(functools.partial(kernel, sizes), out_shape=pltpu.VMEM((2,...]
where the time goes in v3:
time: 26.7 us; the launch traced here: 26.5 us
  Pallas kernels  25.9 us (97%)
  between operations  0.64 us (2%)
    pallas_call x1, Pallas kernels, per_device(): pl.pallas_call(functools.partial(kernel, sizes), out_shape=pltpu.VMEM((2,...  25.2 us
    pallas_call x1, Pallas kernels, per_device(): pl.pallas_call(put_out, out_shape=(shape, shape), in_specs=[pl.BlockSpec(...  0.69 us

profile of v3, /device:TPU:1, one launch (start us, length us, event | category | flops | bytes accessed | tf_op | source)
XLA Modules:
  0.0 26.5 jit_solution(4465769571298199351)
XLA Ops:
  0.6 25.2 %shard_map.68.tiles = f32[2,128,128]{2,1,0:T(8,128)S(1)} custom-call(f32[64,256]{1,0:T(8,128)} %refs_0_.1, f32[64,256]{1,0:T(8,128)} %refs_1_.1, f32[64,256]{1,0:T(8,128)} %refs_2_.1, f32[64,256]{1,0:T(8,128)} %refs_3_.1, f32[64,256]{1,0:T(8,128)} %refs_4_.1), custom_call_target="tpu_custom_call" | custom-call | tf_op jit(solution)/shard_map/pallas_call | solution.py:389
  25.9 0.7 %shard_map.69 = (f32[64,256]{1,0:T(8,128)}, f32[64,256]{1,0:T(8,128)}) custom-call(f32[2,128,128]{2,1,0:T(8,128)S(1)} %shard_map.68.tiles), custom_call_target="tpu_custom_call" | custom-call | tf_op jit(solution)/shard_map/pallas_call | solution.py:418

commit v4 on v3

--- a/solution.py
+++ b/solution.py
@@ -1,4 +1,5 @@
 import functools
+import itertools
 
 import jax
 import jax.numpy as jnp
@@ -35,7 +36,7 @@
         6:17
     ]
     (gathered, share) = refs[17:19]
-    (load_sem, swap_sem, halo_send, halo_recv, mirror_sem, send_sem, recv_sem) = refs[19:]
+    (load_sem, swap_sem, halo_send, halo_recv, mirror_sem, send_sem, recv_sem, round_sem) = refs[19:]
     devices = 1
     for a in AXES:
         devices *= sizes[a]
@@ -73,10 +74,20 @@
             )
             loads[-1].start()
     barrier = pltpu.get_barrier_semaphore()
-    for o in range(1, devices):
-        pl.semaphore_signal(
-            barrier, inc=1, device_id=lax.bitwise_and(me + o, devices - 1), device_id_type=LOGICAL
-        )
+    peers = []
+    for axes in (("gx", "gy_2"), ("gy_1",), ("gy_0",)):
+        for offset in itertools.product(*[range(sizes[a]) for a in axes]):
+            if any(offset):
+                peers.append({a: lax.rem(place[a] + o, sizes[a]) for a, o in zip(axes, offset)})
+    neighbours = [at(right, 0), at(right, 1), at(left, 0), at(left, 1)]
+
+    def greet(devices_to, semaphore):
+        for device in devices_to:
+            pl.semaphore_signal(
+                semaphore, inc=1, device_id=device, device_id_type=pl.DeviceIdType.MESH
+            )
+
+    greet(neighbours + peers, barrier)
     for load in loads:
         load.wait()
 
@@ -103,7 +114,8 @@
                 value = jnp.where(inside, moved, value)
             pack[side, pl.ds(64 + 8 * i, 8), :] = value
 
-    pl.semaphore_wait(barrier, devices - 1)
+    pl.semaphore_wait(barrier, len(neighbours) + len(peers))
+    greet(peers, round_sem.at[0])
 
     swap = pltpu.make_async_remote_copy(
         block.at[:, :, pl.ds(0, 64), :],
@@ -169,6 +181,8 @@
 
     swap.wait()
     build(1 - core, 96 * core, lambda a, strided: block[a, far, strided, :])
+    pl.semaphore_wait(round_sem.at[0], len(peers))
+    greet(peers, round_sem.at[1])
 
     for part, ref, count in ((0, halo, 64), (1, halo_b, 16)):
         for half in range(2):
@@ -264,6 +278,8 @@
         line = jnp.sum(packed[4 * r : 4 * r + 4, :], axis=0, keepdims=True)
         share[r : r + 1, :] = line
         gathered[me, r : r + 1, :] = line
+
+    pl.semaphore_wait(round_sem.at[1], len(peers))
 
     for o in range(1, devices):
         pltpu.make_async_remote_copy(
@@ -412,6 +428,7 @@
             dma((2,)),
             dma,
             dma,
+            pltpu.SemaphoreType.REGULAR((2,)),
         ],
         compiler_params=pltpu.CompilerParams(collective_id=0, has_side_effects=True),
     )(*arrays)

time: 26.7 us -> 25.8 us (0.966)
  Pallas kernels: 25.9 us -> 25 us
    pallas_call x1, Pallas kernels: 25.2 us -> 24.3 us  [per_device(): pl.pallas_call(functools.partial(kernel, sizes), out_shape=pltpu.VMEM((2,...]
where the time goes in v4:
time: 25.8 us; the launch traced here: 25.6 us
  Pallas kernels  25 us (97%)
  between operations  0.64 us (2%)
    pallas_call x1, Pallas kernels, per_device(): pl.pallas_call(functools.partial(kernel, sizes), out_shape=pltpu.VMEM((2,...  24.3 us
    pallas_call x1, Pallas kernels, per_device(): pl.pallas_call(put_out, out_shape=(shape, shape), in_specs=[pl.BlockSpec(...  0.69 us

profile of v4, /device:TPU:1, one launch (start us, length us, event | category | flops | bytes accessed | tf_op | source)
XLA Modules:
  0.0 25.6 jit_solution(11389800370123526460)
XLA Ops:
  0.6 24.3 %shard_map.68.tiles = f32[2,128,128]{2,1,0:T(8,128)S(1)} custom-call(f32[64,256]{1,0:T(8,128)} %refs_0_.1, f32[64,256]{1,0:T(8,128)} %refs_1_.1, f32[64,256]{1,0:T(8,128)} %refs_2_.1, f32[64,256]{1,0:T(8,128)} %refs_3_.1, f32[64,256]{1,0:T(8,128)} %refs_4_.1), custom_call_target="tpu_custom_call" | custom-call | tf_op jit(solution)/shard_map/pallas_call | solution.py:405
  24.9 0.7 %shard_map.69 = (f32[64,256]{1,0:T(8,128)}, f32[64,256]{1,0:T(8,128)}) custom-call(f32[2,128,128]{2,1,0:T(8,128)S(1)} %shard_map.68.tiles), custom_call_target="tpu_custom_call" | custom-call | tf_op jit(solution)/shard_map/pallas_call | solution.py:435

commit v5 on v4

--- a/solution.py
+++ b/solution.py
@@ -32,18 +32,19 @@
 def kernel(sizes, *refs):
     inputs = refs[:5]
     out = refs[5]
-    (block, pack, halo, halo_b, edge_b, coef, field, basis, merged, mirror, gram_parts) = refs[
-        6:17
-    ]
-    (gathered, share) = refs[17:19]
-    (load_sem, swap_sem, halo_send, halo_recv, mirror_sem, send_sem, recv_sem, round_sem) = refs[19:]
+    (block, pack_r, pack_l, halo_r, halo_rb, halo_l, halo_lb, edge_b) = refs[6:14]
+    (coef, field, basis, merged, mirror, joined, gram_parts) = refs[14:21]
+    (gathered, share) = refs[21:23]
+    (load_sem, swap_sem, right_send, right_recv, left_send, left_recv) = refs[23:29]
+    (mirror_sem, tail_sem, send_sem, recv_sem, round_sem) = refs[29:]
     devices = 1
     for a in AXES:
         devices *= sizes[a]
 
     place = {a: lax.axis_index(a) for a in AXES}
     core = place["gx"]
-    sibling = {"gx": 1 - core}
+    far = 1 - core
+    sibling = {"gx": far}
 
     def along(step):
         total = sizes["gy_0"] * sizes["gy_1"] * sizes["gy_2"]
@@ -94,29 +95,46 @@
     lane = lax.broadcasted_iota(jnp.int32, (8, 128), 1)
     row = lax.broadcasted_iota(jnp.int32, (8, 128), 0)
 
+    for n, (first, second) in enumerate(((X0, RE), (VX, VY), (B, B))):
+        count = 64 if first != B else 32
+        for i in range(count // 8):
+            other = 8 * i if first != B else 32 + 8 * i
+            pack_r[pl.ds(64 * n + 8 * i, 8), :] = jnp.where(
+                lane >= 64,
+                block[first, 1, pl.ds(8 * i, 8), :],
+                pltpu.roll(block[second, 1, pl.ds(other, 8), :], 64, 1),
+            )
+
+    def pack_left(place_at, piece):
+        value = piece(0)
+        for g in range(1, GROUPS):
+            inside = (lane >= DEPTH * g) & (lane < DEPTH * (g + 1))
+            value = jnp.where(inside, pltpu.roll(piece(g), DEPTH * g, 1), value)
+        pack_l[pl.ds(place_at, 8), :] = value
+
     for i in range(8):
-        rows = pl.ds(8 * i, 8)
-        for side, tile, first in ((0, 1, 96), (1, 0, 0)):
-            value = block[PACKED[0], tile, rows, :]
-            for g in range(1, GROUPS):
-                start = (first + DEPTH * g) % 128
-                moved = pltpu.roll(block[PACKED[g], tile, rows, :], DEPTH * g, 1)
-                inside = (lane >= start) & (lane < start + DEPTH)
-                value = jnp.where(inside, moved, value)
-            pack[side, rows, :] = value
+        pack_left(8 * i, lambda g: block[PACKED[g], 0, pl.ds(8 * i, 8), :])
     for i in range(2):
-        for side, tile, first in ((0, 1, 96), (1, 0, 0)):
-            value = block[B, tile, pl.ds(8 * i, 8), :]
-            for g in range(1, GROUPS):
-                start = (first + DEPTH * g) % 128
-                moved = pltpu.roll(block[B, tile, pl.ds(16 * g + 8 * i, 8), :], DEPTH * g, 1)
-                inside = (lane >= start) & (lane < start + DEPTH)
-                value = jnp.where(inside, moved, value)
-            pack[side, pl.ds(64 + 8 * i, 8), :] = value
+        pack_left(64 + 8 * i, lambda g: block[B, 0, pl.ds(16 * g + 8 * i, 8), :])
 
     pl.semaphore_wait(barrier, len(neighbours) + len(peers))
     greet(peers, round_sem.at[0])
 
+    sends = []
+    for n in range(3):
+        count = 64 if n < 2 else 32
+        rows = pl.ds(pl.multiple_of(count * core, count), count)
+        sends.append(
+            pltpu.make_async_remote_copy(
+                pack_r.at[pl.ds(64 * n, count), :],
+                halo_r.at[n, rows, :] if n < 2 else halo_rb.at[rows, :],
+                right_send.at[n],
+                right_recv.at[n, core],
+                device_id=at(right, 0),
+                device_id_type=pl.DeviceIdType.MESH,
+            )
+        )
+        sends[-1].start()
     swap = pltpu.make_async_remote_copy(
         block.at[:, :, pl.ds(0, 64), :],
         block.at[:, :, pl.ds(64, 64), :],
@@ -126,27 +144,31 @@
         device_id_type=pl.DeviceIdType.MESH,
     )
     swap.start()
-    sends = []
-    for side, chip, target in ((0, right, 0), (1, left, 1)):
-        same = core if target == 0 else 1 - core
-        for part in range(2):
-            if part == 0:
-                source = pack.at[side, pl.ds(0, 64), :]
-                landing = halo.at[pl.ds(pl.multiple_of(64 * same, 64), 64), :]
-            else:
-                source = pack.at[side, pl.ds(64, 16), :]
-                landing = halo_b.at[pl.ds(pl.multiple_of(16 * same, 16), 16), :]
-            copy = pltpu.make_async_remote_copy(
-                source,
-                landing,
-                halo_send.at[side, part],
-                halo_recv.at[part, same],
-                device_id=at(chip, target),
+    for n in range(2):
+        count = 64 if n == 0 else 16
+        rows = pl.ds(pl.multiple_of(count * far, count), count)
+        sends.append(
+            pltpu.make_async_remote_copy(
+                pack_l.at[pl.ds(64 * n, count), :],
+                halo_l.at[rows, :] if n == 0 else halo_lb.at[rows, :],
+                left_send.at[n],
+                left_recv.at[n, far],
+                device_id=at(left, 1),
                 device_id_type=pl.DeviceIdType.MESH,
             )
-            copy.start()
-            sends.append(copy)
-    far = 1 - core
+        )
+        sends[-1].start()
+
+    def arrived(landing, sem):
+        pltpu.make_async_remote_copy(
+            landing,
+            landing,
+            sem,
+            sem,
+            device_id=sibling,
+            device_id_type=pl.DeviceIdType.MESH,
+        ).wait_recv()
+
     inv = 1.0 / SCALE
 
     def row_shift(load, t):
@@ -159,12 +181,16 @@
     def column_shift(value, offset):
         return pltpu.roll(value, (-offset) % 128, 1)
 
-    def build(q, first, edge):
-        inside = (lane >= first) & (lane < first + DEPTH)
+    def fill(q, inside, edge):
         for a in range(5):
             for t in range(STEPS):
                 strided = pl.ds(t, 8, stride=STEPS)
-                field[a, q, t] = jnp.where(inside, edge(a, strided), block[a, core, strided, :])
+                value = block[a, core, strided, :]
+                if inside is not None:
+                    value = jnp.where(inside, edge(a, strided), value)
+                field[a, q, t] = value
+
+    def build(q):
         for t in range(STEPS):
             speed = lambda i: field[VX, q, i]
             here = speed(t)
@@ -180,36 +206,39 @@
             coef[8, q, t] = (here + column_shift(here, -2)) * (inv / 24.0) + inv / 12.0
 
     swap.wait()
-    build(1 - core, 96 * core, lambda a, strided: block[a, far, strided, :])
+    fill(1, None, None)
+    build(1)
     pl.semaphore_wait(round_sem.at[0], len(peers))
     greet(peers, round_sem.at[1])
 
-    for part, ref, count in ((0, halo, 64), (1, halo_b, 16)):
-        for half in range(2):
-            landing = ref.at[pl.ds(count * half, count), :]
-            pltpu.make_async_remote_copy(
-                landing,
-                landing,
-                halo_send.at[0, part],
-                halo_recv.at[part, half],
-                device_id=sibling,
-                device_id_type=pl.DeviceIdType.MESH,
-            ).wait_recv()
-    for s in range(8):
-        for i in range(2):
-            value = halo_b[pl.ds(16 * (s // 4) + 8 * i, 8), :]
-            if s % 4:
-                value = pltpu.roll(value, 128 - DEPTH * (s % 4), 1)
-            edge_b[pl.ds(16 * s + 8 * i, 8), :] = value
-
-    def from_chip(a, strided):
-        if a == B:
-            return edge_b[strided, :]
-        g = PACKED.index(a)
-        edge = halo[strided, :]
-        return pltpu.roll(edge, 128 - DEPTH * g, 1) if g else edge
-
-    build(core, 96 * (1 - core), from_chip)
+    @pl.when(core == 1)
+    def _():
+        fill(0, lane >= 64, lambda a, strided: block[a, 0, strided, :])
+
+    @pl.when(core == 0)
+    def _():
+        for n in range(3):
+            for half in range(2):
+                if n < 2:
+                    arrived(halo_r.at[n, pl.ds(64 * half, 64), :], right_recv.at[n, half])
+                else:
+                    arrived(halo_rb.at[pl.ds(32 * half, 32), :], right_recv.at[n, half])
+        for s in range(8):
+            for i in range(2):
+                value = halo_rb[pl.ds(32 * (s // 4) + 16 * (s % 2) + 8 * i, 8), :]
+                if s % 4 >= 2:
+                    value = pltpu.roll(value, 64, 1)
+                edge_b[pl.ds(16 * s + 8 * i, 8), :] = value
+
+        def from_left(a, strided):
+            if a == B:
+                return edge_b[strided, :]
+            edge = halo_r[0 if a in (X0, RE) else 1, strided, :]
+            return edge if a in (X0, VX) else pltpu.roll(edge, 64, 1)
+
+        fill(0, lane >= 64, from_left)
+
+    build(0)
 
     def operate(load, q, t):
         here = load(t)
@@ -224,7 +253,7 @@
         value += coef[8, q, t] * column_shift(here, -2)
         return value
 
-    own_left = lane < 64
+    middle = (lane >= 32) & (lane < 96)
     for t in range(STEPS):
         parts = []
         for q in range(2):
@@ -232,7 +261,7 @@
             basis[0, q, t] = jnp.zeros((8, 128), jnp.float32)
             parts.append(field[B, q, t] - SCALE * operate(load, q, t) - SHIFT * load(t))
             basis[1, q, t] = parts[q]
-        merged[0, t] = jnp.where(own_left, parts[0], parts[1])
+        merged[0, t] = jnp.where(middle, parts[1], parts[0])
 
     def grow(k, carry):
         for t in range(STEPS):
@@ -241,7 +270,7 @@
                 load = lambda i: basis[k + 1, q, i]
                 parts.append(operate(load, q, t) - basis[k, q, t])
                 basis[k + 2, q, t] = parts[q]
-            merged[k + 1, t] = jnp.where(own_left, parts[0], parts[1])
+            merged[k + 1, t] = jnp.where(middle, parts[1], parts[0])
         return carry
 
     lax.fori_loop(0, RESTART, grow, 0, unroll=RESTART)
@@ -299,6 +328,72 @@
         device_id_type=pl.DeviceIdType.MESH,
     )
     mirror_copy.start()
+
+    tail = basis.at[pl.ds(1, VECTORS), 2]
+    tail_copy = pltpu.make_async_remote_copy(
+        tail,
+        tail,
+        tail_sem.at[0],
+        tail_sem.at[1],
+        device_id=sibling,
+        device_id_type=pl.DeviceIdType.MESH,
+    )
+
+    @pl.when(core == 1)
+    def _():
+        for n in range(2):
+            for half in range(2):
+                if n == 0:
+                    arrived(halo_l.at[pl.ds(64 * half, 64), :], left_recv.at[n, half])
+                else:
+                    arrived(halo_lb.at[pl.ds(16 * half, 16), :], left_recv.at[n, half])
+        for s in range(8):
+            for i in range(2):
+                value = halo_lb[pl.ds(16 * (s // 4) + 8 * i, 8), :]
+                if s % 4:
+                    value = pltpu.roll(value, 128 - DEPTH * (s % 4), 1)
+                edge_b[pl.ds(16 * s + 8 * i, 8), :] = value
+
+        def from_right(a, strided):
+            if a == B:
+                return edge_b[strided, :]
+            g = PACKED.index(a)
+            edge = halo_l[strided, :]
+            return pltpu.roll(edge, 128 - DEPTH * g, 1) if g else edge
+
+        fill(2, lane < DEPTH, from_right)
+        build(2)
+        for t in range(STEPS):
+            load = lambda i: field[X0, 2, i]
+            basis[0, 2, t] = jnp.zeros((8, 128), jnp.float32)
+            basis[1, 2, t] = field[B, 2, t] - SCALE * operate(load, 2, t) - SHIFT * load(t)
+
+        def grow_tail(k, carry):
+            for t in range(STEPS):
+                load = lambda i: basis[k + 1, 2, i]
+                basis[k + 2, 2, t] = operate(load, 2, t) - basis[k, 2, t]
+            return carry
+
+        lax.fori_loop(0, RESTART, grow_tail, 0, unroll=3)
+        tail_copy.start()
+
+    mirror_copy.wait()
+
+    @pl.when(core == 0)
+    def _():
+        tail_copy.wait_recv()
+
+    upper = lane < 96
+    near = row < 4
+    is_first = (row * 0 + core) == 0
+    in_first = near == is_first
+    for k in range(VECTORS):
+        for t in range(STEPS):
+            own, other = merged[k, t], mirror[k, t]
+            second = pltpu.roll(jnp.where(is_first, other, own), 4, 0)
+            last = jnp.where(in_first, second, basis[k + 1, 2, t])
+            joined[k, t] = jnp.where(upper, jnp.where(near, own, other), last)
+
     others = gathered.at[pl.ds(0, devices - 1)]
     everyone = pltpu.make_async_remote_copy(
         others, others, send_sem, recv_sem, device_id=sibling, device_id_type=pl.DeviceIdType.MESH
@@ -310,7 +405,6 @@
         jnp.broadcast_to(summed[0:1, :], (8, 128)),
         jnp.broadcast_to(summed[1:2, :], (8, 128)),
     )
-    mirror_copy.wait()
 
     values = values_at_zero()
     columns = []
@@ -360,13 +454,12 @@
 
     for t in range(STEPS):
         strided = pl.ds(t, 8, stride=STEPS)
-        near = row < 4
         answer = jnp.where(
             near, block[X0, core, strided, :], pltpu.roll(block[X0, far, strided, :], 4, 0)
         )
         residual = jnp.zeros((8, 128), jnp.float32)
         for k in range(VECTORS):
-            cells = jnp.where(near, merged[k, t], mirror[k, t])
+            cells = joined[k, t]
             residual = residual + left_over[k] * cells
             if k < RESTART:
                 answer = answer + weights[k] * cells
@@ -374,6 +467,11 @@
         out[1, strided, :] = residual
 
     everyone.wait_send()
+
+    @pl.when(core == 1)
+    def _():
+        tail_copy.wait_send()
+
     for copy in sends:
         copy.wait_send()
 
@@ -409,13 +507,17 @@
         out_specs=pl.BlockSpec(memory_space=pltpu.VMEM),
         scratch_shapes=[
             pltpu.VMEM((5, 2, 128, 128), f32),
-            pltpu.VMEM((2, 80, 128), f32),
+            pltpu.VMEM((160, 128), f32),
+            pltpu.VMEM((80, 128), f32),
+            pltpu.VMEM((2, 128, 128), f32),
+            pltpu.VMEM((64, 128), f32),
             pltpu.VMEM((128, 128), f32),
             pltpu.VMEM((32, 128), f32),
             pltpu.VMEM((128, 128), f32),
-            pltpu.VMEM((9, 2, STEPS, 8, 128), f32),
-            pltpu.VMEM((5, 2, STEPS, 8, 128), f32),
-            pltpu.VMEM((VECTORS + 1, 2, STEPS, 8, 128), f32),
+            pltpu.VMEM((9, 3, STEPS, 8, 128), f32),
+            pltpu.VMEM((5, 3, STEPS, 8, 128), f32),
+            pltpu.VMEM((VECTORS + 1, 3, STEPS, 8, 128), f32),
+            pltpu.VMEM((VECTORS, STEPS, 8, 128), f32),
             pltpu.VMEM((VECTORS, STEPS, 8, 128), f32),
             pltpu.VMEM((VECTORS, STEPS, 8, 128), f32),
             pltpu.VMEM((VECTORS, VECTORS, 128), f32),
@@ -423,8 +525,11 @@
             pltpu.VMEM((2, 128), f32),
             dma((5, 2)),
             dma((2,)),
+            dma((3,)),
+            dma((3, 2)),
+            dma((2,)),
             dma((2, 2)),
-            dma((2, 2)),
+            dma((2,)),
             dma((2,)),
             dma,
             dma,

time: 25.8 us -> 23.6 us (0.915)
  Pallas kernels: 25 us -> 22.7 us
    pallas_call x1, Pallas kernels: 24.3 us -> 22 us  [per_device(): pl.pallas_call(functools.partial(kernel, sizes), out_shape=pltpu.VMEM((2,...]
where the time goes in v5:
time: 23.6 us; the launch traced here: 23.4 us
  Pallas kernels  22.7 us (96%)
  between operations  0.64 us (3%)
    pallas_call x1, Pallas kernels, per_device(): pl.pallas_call(functools.partial(kernel, sizes), out_shape=pltpu.VMEM((2,...  22 us
    pallas_call x1, Pallas kernels, per_device(): pl.pallas_call(put_out, out_shape=(shape, shape), in_specs=[pl.BlockSpec(...  0.69 us

profile of v5, /device:TPU:1, one launch (start us, length us, event | category | flops | bytes accessed | tf_op | source)
XLA Modules:
  0.0 23.4 jit_solution(12780068540106244268)
XLA Ops:
  0.6 22.0 %shard_map.68.tiles = f32[2,128,128]{2,1,0:T(8,128)S(1)} custom-call(f32[64,256]{1,0:T(8,128)} %refs_0_.1, f32[64,256]{1,0:T(8,128)} %refs_1_.1, f32[64,256]{1,0:T(8,128)} %refs_2_.1, f32[64,256]{1,0:T(8,128)} %refs_3_.1, f32[64,256]{1,0:T(8,128)} %refs_4_.1), custom_call_target="tpu_custom_call" | custom-call | tf_op jit(solution)/shard_map/pallas_call | solution.py:503
  22.7 0.7 %shard_map.69 = (f32[64,256]{1,0:T(8,128)}, f32[64,256]{1,0:T(8,128)}) custom-call(f32[2,128,128]{2,1,0:T(8,128)S(1)} %shard_map.68.tiles), custom_call_target="tpu_custom_call" | custom-call | tf_op jit(solution)/shard_map/pallas_call | solution.py:540

commit v6 on v5

--- a/solution.py
+++ b/solution.py
@@ -263,39 +263,33 @@
             basis[1, q, t] = parts[q]
         merged[0, t] = jnp.where(middle, parts[1], parts[0])
 
-    def grow(k, carry):
+    def gram_row(k, others):
+        sums = [None] * len(others)
         for t in range(STEPS):
-            parts = []
-            for q in range(2):
-                load = lambda i: basis[k + 1, q, i]
-                parts.append(operate(load, q, t) - basis[k, q, t])
-                basis[k + 2, q, t] = parts[q]
-            merged[k + 1, t] = jnp.where(middle, parts[1], parts[0])
-        return carry
-
-    lax.fori_loop(0, RESTART, grow, 0, unroll=RESTART)
-
-    size = 4
-    for bi in range(VECTORS // size):
-        for bj in range(bi + 1):
-            pairs = [
-                (i, j)
-                for i in range(bi * size, bi * size + size)
-                for j in range(bj * size, bj * size + size)
-                if j <= i
-            ]
-            sums = {}
+            cells = merged[k, t]
+            for n, j in enumerate(others):
+                product = cells * (cells if j == k else merged[j, t])
+                sums[n] = product if t == 0 else sums[n] + product
+        for n, j in enumerate(others):
+            total = jnp.sum(sums[n], axis=0, keepdims=True)
+            gram_parts[k, j : j + 1, :] = total
+            if j != k:
+                gram_parts[j, k : k + 1, :] = total
+
+    for k in range(VECTORS):
+        chunks = [list(range(j, min(j + 4, k + 1))) for j in range(0, k + 1, 4)]
+        if k < RESTART:
             for t in range(STEPS):
-                need = sorted({i for pair in pairs for i in pair})
-                cells = {i: merged[i, t] for i in need}
-                for i, j in pairs:
-                    product = cells[i] * cells[j]
-                    sums[i, j] = product if t == 0 else sums[i, j] + product
-            for i, j in pairs:
-                total = jnp.sum(sums[i, j], axis=0, keepdims=True)
-                gram_parts[i, j : j + 1, :] = total
-                if i != j:
-                    gram_parts[j, i : i + 1, :] = total
+                parts = []
+                for q in range(2):
+                    load = lambda i: basis[k + 1, q, i]
+                    parts.append(operate(load, q, t) - basis[k, q, t])
+                    basis[k + 2, q, t] = parts[q]
+                merged[k + 1, t] = jnp.where(middle, parts[1], parts[0])
+                if t % 4 == 3 and chunks:
+                    gram_row(k, chunks.pop(0))
+        for chunk in chunks:
+            gram_row(k, chunk)
 
     place_in = lane - 32 * (row & 3)
     packed = jnp.zeros((8, 128), jnp.float32)
@@ -310,18 +304,21 @@
 
     pl.semaphore_wait(round_sem.at[1], len(peers))
 
-    for o in range(1, devices):
+    half = devices // 2
+    mine = lax.rem(me, half) * 2 + core
+    for o in range(devices - 1):
+        chip = o + jnp.where(mine <= o, 1, 0)
         pltpu.make_async_remote_copy(
             share,
             gathered.at[me],
             send_sem,
             recv_sem,
-            device_id=lax.bitwise_and(me + o, devices - 1),
+            device_id=lax.bitwise_and(chip, 1) * half + lax.shift_right_logical(chip, 1),
             device_id_type=LOGICAL,
         ).start()
     mirror_copy = pltpu.make_async_remote_copy(
-        merged,
-        mirror,
+        merged.at[:, :, pl.ds(4, 4), :],
+        mirror.at[:, :, pl.ds(4, 4), :],
         mirror_sem.at[0],
         mirror_sem.at[1],
         device_id=sibling,
@@ -329,7 +326,7 @@
     )
     mirror_copy.start()
 
-    tail = basis.at[pl.ds(1, VECTORS), 2]
+    tail = basis.at[pl.ds(1, VECTORS), 2, :, pl.ds(4, 4), :]
     tail_copy = pltpu.make_async_remote_copy(
         tail,
         tail,

time: 23.6 us -> 22.9 us (0.970)
  Pallas kernels: 22.7 us -> 22 us
    pallas_call x1, Pallas kernels: 22 us -> 21.3 us  [per_device(): pl.pallas_call(functools.partial(kernel, sizes), out_shape=pltpu.VMEM((2,...]
where the time goes in v6:
time: 22.9 us; the launch traced here: 22.7 us
  Pallas kernels  22 us (96%)
  between operations  0.64 us (3%)
    pallas_call x1, Pallas kernels, per_device(): pl.pallas_call(functools.partial(kernel, sizes), out_shape=pltpu.VMEM((2,...  21.3 us
    pallas_call x1, Pallas kernels, per_device(): pl.pallas_call(put_out, out_shape=(shape, shape), in_specs=[pl.BlockSpec(...  0.69 us

profile of v6, /device:TPU:1, one launch (start us, length us, event | category | flops | bytes accessed | tf_op | source)
XLA Modules:
  0.0 22.7 jit_solution(1354544796382323506)
XLA Ops:
  0.6 21.3 %shard_map.68.tiles = f32[2,128,128]{2,1,0:T(8,128)S(1)} custom-call(f32[64,256]{1,0:T(8,128)} %refs_0_.1, f32[64,256]{1,0:T(8,128)} %refs_1_.1, f32[64,256]{1,0:T(8,128)} %refs_2_.1, f32[64,256]{1,0:T(8,128)} %refs_3_.1, f32[64,256]{1,0:T(8,128)} %refs_4_.1), custom_call_target="tpu_custom_call" | custom-call | tf_op jit(solution)/shard_map/pallas_call | solution.py:500
  22.0 0.7 %shard_map.69 = (f32[64,256]{1,0:T(8,128)}, f32[64,256]{1,0:T(8,128)}) custom-call(f32[2,128,128]{2,1,0:T(8,128)S(1)} %shard_map.68.tiles), custom_call_target="tpu_custom_call" | custom-call | tf_op jit(solution)/shard_map/pallas_call | solution.py:537

commit v7 on v6

--- a/solution.py
+++ b/solution.py
@@ -33,10 +33,10 @@
     inputs = refs[:5]
     out = refs[5]
     (block, pack_r, pack_l, halo_r, halo_rb, halo_l, halo_lb, edge_b) = refs[6:14]
-    (coef, field, basis, merged, mirror, joined, gram_parts) = refs[14:21]
-    (gathered, share) = refs[21:23]
-    (load_sem, swap_sem, right_send, right_recv, left_send, left_recv) = refs[23:29]
-    (mirror_sem, tail_sem, send_sem, recv_sem, round_sem) = refs[29:]
+    (coef, field, basis, merged, mirror, joined, gram_parts, halves, gram_half) = refs[14:23]
+    (gathered, share) = refs[23:25]
+    (load_sem, swap_sem, right_send, right_recv, left_send, left_recv) = refs[25:31]
+    (mirror_sem, tail_sem, send_sem, recv_sem, round_sem) = refs[31:]
     devices = 1
     for a in AXES:
         devices *= sizes[a]
@@ -205,18 +205,136 @@
             coef[7, q, t] = (here + column_shift(here, 2)) * (-inv / 24.0) + inv / 12.0
             coef[8, q, t] = (here + column_shift(here, -2)) * (inv / 24.0) + inv / 12.0
 
+    def operate(load, q, t):
+        here = load(t)
+        value = coef[0, q, t] * here
+        value += coef[1, q, t] * row_shift(load, t + 1)
+        value += coef[2, q, t] * row_shift(load, t - 1)
+        value += coef[3, q, t] * row_shift(load, t + 2)
+        value += coef[4, q, t] * row_shift(load, t - 2)
+        value += coef[5, q, t] * column_shift(here, 1)
+        value += coef[6, q, t] * column_shift(here, -1)
+        value += coef[7, q, t] * column_shift(here, 2)
+        value += coef[8, q, t] * column_shift(here, -2)
+        return value
+
+    middle = (lane >= 32) & (lane < 96)
+
+    def keep(k, q, values):
+        for t in range(STEPS):
+            basis[k + 1, q, t] = values[t]
+            if q == 0:
+                merged[k, t] = jnp.where(middle, basis[k + 1, 1, t], values[t])
+        for t in range(8):
+            moved = pltpu.roll(values[t + 8], 64, 1)
+            here = values[t]
+            halves[q, k, t] = jnp.where(middle == (q == 1), here, moved)
+
+    def steps(q):
+        load = lambda i: field[X0, q, i]
+        for t in range(STEPS):
+            basis[0, q, t] = jnp.zeros((8, 128), jnp.float32)
+        values = []
+        for t in range(STEPS):
+            values.append(field[B, q, t] - SCALE * operate(load, q, t) - SHIFT * load(t))
+        keep(0, q, values)
+
+        def grow(k, carry):
+            load = lambda i: basis[k + 1, q, i]
+            keep(k + 1, q, [operate(load, q, t) - basis[k, q, t] for t in range(STEPS)])
+            return carry
+
+        lax.fori_loop(0, RESTART, grow, 0, unroll=RESTART)
+
+    def gram(q):
+        size = 4
+        for bi in range(VECTORS // size):
+            for bj in range(bi + 1):
+                pairs = [
+                    (i, j)
+                    for i in range(bi * size, bi * size + size)
+                    for j in range(bj * size, bj * size + size)
+                    if j <= i
+                ]
+                sums = {}
+                for t in range(8):
+                    need = sorted({i for pair in pairs for i in pair})
+                    cells = {i: halves[q, i, t] for i in need}
+                    for i, j in pairs:
+                        product = cells[i] * cells[j]
+                        sums[i, j] = product if t == 0 else sums[i, j] + product
+                for i, j in pairs:
+                    if q == 1:
+                        gram_half[i * (i + 1) // 2 + j] = sums[i, j]
+                        continue
+                    total = sums[i, j] + gram_half[i * (i + 1) // 2 + j]
+                    total = jnp.sum(total, axis=0, keepdims=True)
+                    gram_parts[i, j : j + 1, :] = total
+                    if i != j:
+                        gram_parts[j, i : i + 1, :] = total
+
     swap.wait()
     fill(1, None, None)
     build(1)
     pl.semaphore_wait(round_sem.at[0], len(peers))
     greet(peers, round_sem.at[1])
 
+    def steps_both():
+        for t in range(STEPS):
+            parts = []
+            for q in range(2):
+                load = lambda i: field[X0, q, i]
+                basis[0, q, t] = jnp.zeros((8, 128), jnp.float32)
+                parts.append(field[B, q, t] - SCALE * operate(load, q, t) - SHIFT * load(t))
+                basis[1, q, t] = parts[q]
+            merged[0, t] = jnp.where(middle, parts[1], parts[0])
+
+        def grow(k, carry):
+            for t in range(STEPS):
+                parts = []
+                for q in range(2):
+                    load = lambda i: basis[k + 1, q, i]
+                    parts.append(operate(load, q, t) - basis[k, q, t])
+                    basis[k + 2, q, t] = parts[q]
+                merged[k + 1, t] = jnp.where(middle, parts[1], parts[0])
+            return carry
+
+        lax.fori_loop(0, RESTART, grow, 0, unroll=RESTART)
+
+    def gram_both():
+        size = 4
+        for bi in range(VECTORS // size):
+            for bj in range(bi + 1):
+                pairs = [
+                    (i, j)
+                    for i in range(bi * size, bi * size + size)
+                    for j in range(bj * size, bj * size + size)
+                    if j <= i
+                ]
+                sums = {}
+                for t in range(STEPS):
+                    need = sorted({i for pair in pairs for i in pair})
+                    cells = {i: merged[i, t] for i in need}
+                    for i, j in pairs:
+                        product = cells[i] * cells[j]
+                        sums[i, j] = product if t == 0 else sums[i, j] + product
+                for i, j in pairs:
+                    total = jnp.sum(sums[i, j], axis=0, keepdims=True)
+                    gram_parts[i, j : j + 1, :] = total
+                    if i != j:
+                        gram_parts[j, i : i + 1, :] = total
+
     @pl.when(core == 1)
     def _():
         fill(0, lane >= 64, lambda a, strided: block[a, 0, strided, :])
+        build(0)
+        steps_both()
+        gram_both()
 
     @pl.when(core == 0)
     def _():
+        steps(1)
+        gram(1)
         for n in range(3):
             for half in range(2):
                 if n < 2:
@@ -237,59 +355,9 @@
             return edge if a in (X0, VX) else pltpu.roll(edge, 64, 1)
 
         fill(0, lane >= 64, from_left)
-
-    build(0)
-
-    def operate(load, q, t):
-        here = load(t)
-        value = coef[0, q, t] * here
-        value += coef[1, q, t] * row_shift(load, t + 1)
-        value += coef[2, q, t] * row_shift(load, t - 1)
-        value += coef[3, q, t] * row_shift(load, t + 2)
-        value += coef[4, q, t] * row_shift(load, t - 2)
-        value += coef[5, q, t] * column_shift(here, 1)
-        value += coef[6, q, t] * column_shift(here, -1)
-        value += coef[7, q, t] * column_shift(here, 2)
-        value += coef[8, q, t] * column_shift(here, -2)
-        return value
-
-    middle = (lane >= 32) & (lane < 96)
-    for t in range(STEPS):
-        parts = []
-        for q in range(2):
-            load = lambda i: field[X0, q, i]
-            basis[0, q, t] = jnp.zeros((8, 128), jnp.float32)
-            parts.append(field[B, q, t] - SCALE * operate(load, q, t) - SHIFT * load(t))
-            basis[1, q, t] = parts[q]
-        merged[0, t] = jnp.where(middle, parts[1], parts[0])
-
-    def gram_row(k, others):
-        sums = [None] * len(others)
-        for t in range(STEPS):
-            cells = merged[k, t]
-            for n, j in enumerate(others):
-                product = cells * (cells if j == k else merged[j, t])
-                sums[n] = product if t == 0 else sums[n] + product
-        for n, j in enumerate(others):
-            total = jnp.sum(sums[n], axis=0, keepdims=True)
-            gram_parts[k, j : j + 1, :] = total
-            if j != k:
-                gram_parts[j, k : k + 1, :] = total
-
-    for k in range(VECTORS):
-        chunks = [list(range(j, min(j + 4, k + 1))) for j in range(0, k + 1, 4)]
-        if k < RESTART:
-            for t in range(STEPS):
-                parts = []
-                for q in range(2):
-                    load = lambda i: basis[k + 1, q, i]
-                    parts.append(operate(load, q, t) - basis[k, q, t])
-                    basis[k + 2, q, t] = parts[q]
-                merged[k + 1, t] = jnp.where(middle, parts[1], parts[0])
-                if t % 4 == 3 and chunks:
-                    gram_row(k, chunks.pop(0))
-        for chunk in chunks:
-            gram_row(k, chunk)
+        build(0)
+        steps(0)
+        gram(0)
 
     place_in = lane - 32 * (row & 3)
     packed = jnp.zeros((8, 128), jnp.float32)
@@ -304,16 +372,13 @@
 
     pl.semaphore_wait(round_sem.at[1], len(peers))
 
-    half = devices // 2
-    mine = lax.rem(me, half) * 2 + core
-    for o in range(devices - 1):
-        chip = o + jnp.where(mine <= o, 1, 0)
+    for o in range(1, devices):
         pltpu.make_async_remote_copy(
             share,
             gathered.at[me],
             send_sem,
             recv_sem,
-            device_id=lax.bitwise_and(chip, 1) * half + lax.shift_right_logical(chip, 1),
+            device_id=lax.bitwise_and(me + o, devices - 1),
             device_id_type=LOGICAL,
         ).start()
     mirror_copy = pltpu.make_async_remote_copy(
@@ -518,6 +583,8 @@
             pltpu.VMEM((VECTORS, STEPS, 8, 128), f32),
             pltpu.VMEM((VECTORS, STEPS, 8, 128), f32),
             pltpu.VMEM((VECTORS, VECTORS, 128), f32),
+            pltpu.VMEM((2, VECTORS, 8, 8, 128), f32),
+            pltpu.VMEM((VECTORS * (VECTORS + 1) // 2, 8, 128), f32),
             pltpu.VMEM((devices, 2, 128), f32),
             pltpu.VMEM((2, 128), f32),
             dma((5, 2)),

time: 22.9 us -> 22.7 us (level)
  no operation moved by 1% of the time
where the time goes in v7:
time: 22.7 us; the launch traced here: 22.5 us
  Pallas kernels  21.8 us (96%)
  between operations  0.64 us (3%)
    pallas_call x1, Pallas kernels, per_device(): pl.pallas_call(functools.partial(kernel, sizes), out_shape=pltpu.VMEM((2,...  21.2 us
    pallas_call x1, Pallas kernels, per_device(): pl.pallas_call(put_out, out_shape=(shape, shape), in_specs=[pl.BlockSpec(...  0.69 us

profile of v7, /device:TPU:1, one launch (start us, length us, event | category | flops | bytes accessed | tf_op | source)
XLA Modules:
  0.0 22.5 jit_solution(4665066854463354631)
XLA Ops:
  0.6 21.2 %shard_map.68.tiles = f32[2,128,128]{2,1,0:T(8,128)S(1)} custom-call(f32[64,256]{1,0:T(8,128)} %refs_0_.1, f32[64,256]{1,0:T(8,128)} %refs_1_.1, f32[64,256]{1,0:T(8,128)} %refs_2_.1, f32[64,256]{1,0:T(8,128)} %refs_3_.1, f32[64,256]{1,0:T(8,128)} %refs_4_.1), custom_call_target="tpu_custom_call" | custom-call | tf_op jit(solution)/shard_map/pallas_call | solution.py:565
  21.8 0.7 %shard_map.69 = (f32[64,256]{1,0:T(8,128)}, f32[64,256]{1,0:T(8,128)}) custom-call(f32[2,128,128]{2,1,0:T(8,128)S(1)} %shard_map.68.tiles), custom_call_target="tpu_custom_call" | custom-call | tf_op jit(solution)/shard_map/pallas_call | solution.py:604

commit v8 on v7

--- a/solution.py
+++ b/solution.py
@@ -201,9 +201,9 @@
             coef[4, q, t] = (here + row_shift(speed, t - 2)) * (inv / 24.0) + inv / 12.0
             here = field[VY, q, t]
             coef[5, q, t] = (here + column_shift(here, 1)) * (inv / 3.0) - 4.0 / 3.0 * inv
-            coef[6, q, t] = (here + column_shift(here, -1)) * (-inv / 3.0) - 4.0 / 3.0 * inv
+            coef[6, q, t] = (here + column_shift(here, 1)) * (-inv / 3.0) - 4.0 / 3.0 * inv
             coef[7, q, t] = (here + column_shift(here, 2)) * (-inv / 24.0) + inv / 12.0
-            coef[8, q, t] = (here + column_shift(here, -2)) * (inv / 24.0) + inv / 12.0
+            coef[8, q, t] = (here + column_shift(here, 2)) * (inv / 24.0) + inv / 12.0
 
     def operate(load, q, t):
         here = load(t)
@@ -213,9 +213,9 @@
         value += coef[3, q, t] * row_shift(load, t + 2)
         value += coef[4, q, t] * row_shift(load, t - 2)
         value += coef[5, q, t] * column_shift(here, 1)
-        value += coef[6, q, t] * column_shift(here, -1)
+        value += column_shift(coef[6, q, t] * here, -1)
         value += coef[7, q, t] * column_shift(here, 2)
-        value += coef[8, q, t] * column_shift(here, -2)
+        value += column_shift(coef[8, q, t] * here, -2)
         return value
 
     middle = (lane >= 32) & (lane < 96)

time: 22.7 us -> 22.7 us (level)
  no operation moved by 1% of the time
where the time goes in v8:
time: 22.7 us; the launch traced here: 22.5 us
  Pallas kernels  21.9 us (96%)
  between operations  0.64 us (3%)
    pallas_call x1, Pallas kernels, per_device(): pl.pallas_call(functools.partial(kernel, sizes), out_shape=pltpu.VMEM((2,...  21.2 us
    pallas_call x1, Pallas kernels, per_device(): pl.pallas_call(put_out, out_shape=(shape, shape), in_specs=[pl.BlockSpec(...  0.69 us

profile of v8, /device:TPU:1, one launch (start us, length us, event | category | flops | bytes accessed | tf_op | source)
XLA Modules:
  0.0 22.5 jit_solution(11035141735421088962)
XLA Ops:
  0.6 21.2 %shard_map.68.tiles = f32[2,128,128]{2,1,0:T(8,128)S(1)} custom-call(f32[64,256]{1,0:T(8,128)} %refs_0_.1, f32[64,256]{1,0:T(8,128)} %refs_1_.1, f32[64,256]{1,0:T(8,128)} %refs_2_.1, f32[64,256]{1,0:T(8,128)} %refs_3_.1, f32[64,256]{1,0:T(8,128)} %refs_4_.1), custom_call_target="tpu_custom_call" | custom-call | tf_op jit(solution)/shard_map/pallas_call | solution.py:565
  21.8 0.7 %shard_map.69 = (f32[64,256]{1,0:T(8,128)}, f32[64,256]{1,0:T(8,128)}) custom-call(f32[2,128,128]{2,1,0:T(8,128)S(1)} %shard_map.68.tiles), custom_call_target="tpu_custom_call" | custom-call | tf_op jit(solution)/shard_map/pallas_call | solution.py:604
